TPU v7x, 64 devices: a 2x2x8 block of a 4x4x8 slice. The times are simulated.
64 devices in a mesh: dp: 4 (over x, y), tp: 16 (over z, core).
Axes of the slice: x: 2, y: 2, z: 8, core: 2. Of those that a mesh axis runs over, the one named last changes fastest.
The devices are a block of a 4x4x8 slice.
Arguments:
- token_ids: int32 [65536], P('dp'), parts along dimension 0
- embed_table: bfloat16 [152064, 128], P('tp')
- norm_gain: bfloat16 [128], replicated
- w_up: bfloat16 [128, 18944], P(None, 'tp')
- w_down: bfloat16 [18944, 128], P('tp')
- d_out: bfloat16 [65536, 128], P(('dp', 'tp')), parts along dimension 0
Outputs:
- output 1: bfloat16 [65536, 128], P(('dp', 'tp')), parts along dimension 0
- output 2: float32 [608256, 128], P(('dp', 'tp')), parts along dimension 0
- output 3: float32 [512, 18944], P('dp', 'tp'), parts along dimension 0
- output 4: float32 [75776, 128], P(('dp', 'tp')), parts along dimension 0
There are 4 independent parts. A program takes and returns all parts, laid end to end along the dimension named above; an argument that names none is the same for every part.
All inputs are finite; a program needn't handle non-finite values.
Results may differ from a plain program's by a relative error of at most 0.00933744.
Values are sent between devices in bfloat16 or wider.
A program may use at most 768 MiB of HBM per device.

v0:
```python
import jax
import jax.numpy as jnp
from jax import lax
from jax.sharding import PartitionSpec as P

NORM_EPS = 1e-6


def gelu_tanh(values):
    return jax.nn.gelu(values, approximate=True)


def solution(mesh):
    def shard_body(token_ids, embed_table, norm_gain, w_up, w_down, d_out):
        shard_rows = embed_table.shape[0]
        my_rank = lax.axis_index("tp")
        local_ids = token_ids - my_rank * shard_rows
        is_owned = (local_ids >= 0) & (local_ids < shard_rows)
        safe_ids = jnp.where(is_owned, local_ids, 0)
        lookup_rows = jnp.take(embed_table, safe_ids, axis=0)
        lookup_rows = jnp.where(is_owned[:, None], lookup_rows, jnp.zeros_like(lookup_rows))
        embed_rows = lax.psum_scatter(lookup_rows, "tp", scatter_dimension=0, tiled=True)
        embed_f32 = embed_rows.astype(jnp.float32)
        inv_rms = lax.rsqrt(jnp.mean(embed_f32 * embed_f32, axis=-1, keepdims=True) + NORM_EPS)
        gain_f32 = norm_gain.astype(jnp.float32)
        normed = (embed_f32 * inv_rms * gain_f32).astype(jnp.bfloat16)
        normed_all = lax.all_gather(normed, "tp", axis=0, tiled=True)
        up_act = jnp.dot(normed_all, w_up, preferred_element_type=jnp.float32).astype(jnp.bfloat16)
        hid_f32, gelu_vjp = jax.vjp(gelu_tanh, up_act.astype(jnp.float32))
        hid_act = hid_f32.astype(jnp.bfloat16)
        mlp_part = jnp.dot(hid_act, w_down, preferred_element_type=jnp.float32)
        mlp_out = lax.psum_scatter(mlp_part, "tp", scatter_dimension=0, tiled=True)
        block_out = (embed_f32 + mlp_out).astype(jnp.bfloat16)

        grad_all = lax.all_gather(d_out, "tp", axis=0, tiled=True)
        d_hid = jnp.einsum("td,fd->tf", grad_all, w_down, preferred_element_type=jnp.float32)
        d_up_act = gelu_vjp(d_hid)[0].astype(jnp.bfloat16)
        grad_down = jnp.einsum("tf,td->fd", hid_act, grad_all, preferred_element_type=jnp.float32)
        grad_up = jnp.einsum("td,tf->df", normed_all, d_up_act, preferred_element_type=jnp.float32)
        d_norm_part = jnp.einsum("tf,df->td", d_up_act, w_up, preferred_element_type=jnp.float32)
        d_norm = lax.psum_scatter(d_norm_part, "tp", scatter_dimension=0, tiled=True)
        d_scaled = d_norm * gain_f32
        mean_term = jnp.mean(embed_f32 * d_scaled, axis=-1, keepdims=True)
        d_embed = inv_rms * (d_scaled - embed_f32 * inv_rms * inv_rms * mean_term)
        d_embed = (d_out.astype(jnp.float32) + d_embed).astype(jnp.bfloat16)
        d_embed_all = lax.all_gather(d_embed, "tp", axis=0, tiled=True)
        scatter_ids = jnp.where(is_owned, local_ids, shard_rows)
        grad_table = jax.ops.segment_sum(d_embed_all.astype(jnp.float32), scatter_ids, num_segments=shard_rows)
        return block_out, grad_table, grad_up, grad_down

    return jax.shard_map(
        shard_body,
        mesh=mesh,
        in_specs=(P("dp"), P("tp", None), P(), P(None, "tp"), P("tp", None), P(("dp", "tp"), None)),
        out_specs=(P(("dp", "tp"), None), P(("dp", "tp"), None), P("dp", "tp"), P(("dp", "tp"), None)),
        check_vma=False,
    )
```

profile of v0, /device:TPU:21, one launch (start us, length us, event | category | flops | bytes accessed | tf_op | source)
XLA Modules:
  0.0 579.0 jit_solution(5455316915729950073)
XLA Ops:
  7.2 0.0 copy-start
  7.2 0.0 copy-start.12
  7.2 0.0 copy-start.4
  7.2 0.1 reduce-scatter.4.cloned.1.call-start
  7.3 1.0 compare_and_fusion.1
  8.3 1.5 subtract_select_fusion
  9.8 0.0 copy-done
  9.8 58.0 %gather_fusion = bf16[16384,128]{1,0:T(8,128)(2,1)} fusion(bf16[9504,128]{1,0:T(8,128)(2,1)S(1)} %copy-done, s32[16384]{0:T(1024)S(1)} %get-tuple-element.7), kind=kCustom, calls=%fused_computation | custom fusion | bytes 8454144 | tf_op jit(solution)/shard_map/jit(_take)/gather | solution.py:20
  67.8 13.9 %select_select_fusion = bf16[16384,128]{1,0:T(8,128)(2,1)} fusion(bf16[16384,128]{1,0:T(8,128)(2,1)} %gather_fusion, pred[16384]{0:T(1024)(128)(4,1)S(1)} %get-tuple-element.9, pred[16384]{0:T(1024)(128)(4,1)S(1)} %get-tuple-element.8), kind=kLoop, calls=%fused_computation.20 | loop fusion | flops 4194304 | bytes 8421376 | tf_op jit(solution)/shard_map/jit(_where)/select_n | solution.py:21
  81.7 0.1 reduce-scatter.4.cloned.1.call-update
  81.8 0.1 all-gather.4.cloned.1.call-start
  81.8 0.0 copy-done.12
  81.9 0.0 copy-start.9
  81.9 61.6 %reduce-scatter.4.cloned.1.call-done = bf16[1024,128]{1,0:T(8,128)(2,1)} async-done(((bf16[16384,128]{1,0:T(8,128)(2,1)}), bf16[1024,128]{1,0:T(8,128)(2,1)}) %reduce-scatter.4.cloned.1.call-update) | async-done | bytes 262160 | tf_op jit(solution)/shard_map/reduce_scatter | solution.py:22
  143.4 1.2 fusion.21
  144.6 0.0 copy-start.7
  144.6 1.9 fusion.15
  146.5 0.1 all-gather.4.cloned.1.call-update
  146.6 0.1 all-gather.6.cloned.1.call-start
  146.6 0.7 all-gather.6.cloned.1.call-update
  147.4 0.0 copy-start.6
  147.4 0.1 reduce-scatter.8.cloned.1.call-start
  147.4 40.0 %all-gather.4.cloned.1.call-done = bf16[16384,128]{1,0:T(8,128)(2,1)} async-done(((bf16[1024,128]{1,0:T(8,128)(2,1)}), bf16[16384,128]{1,0:T(8,128)(2,1)}) %all-gather.4.cloned.1.call-update) | async-done | bytes 4194320 | tf_op jit(solution)/shard_map/all_gather | solution.py:27
  187.4 0.0 copy-done.4
  187.4 37.5 %fusion.7 = (bf16[16384,1184]{0,1:T(8,128)(2,1)}, bf16[16384,1184]{0,1:T(8,128)(2,1)}) fusion(bf16[16384,128]{1,0:T(8,128)(2,1)} %all-gather.4.cloned.1.call-done, bf16[128,1184]{0,1:T(8,128)(2,1)S(1)} %copy-done.4), kind=kOutput, calls=%fused_computation.14 | convolution fusion | flops 5179441152 | bytes 82092032 | tf_op jit(solution)/shard_map/dot_general | solution.py:28
  224.9 0.0 copy-done.9
  224.9 1.1 all-gather.6.cloned.1.call-done
  226.0 61.1 %fusion.3 = bf16[16384,1184]{0,1:T(8,128)(2,1)} fusion(bf16[16384,1184]{0,1:T(8,128)(2,1)} %get-tuple-element.11, bf16[16384,128]{1,0:T(8,128)(2,1)} %all-gather.6.cloned.1.call-done, bf16[1184,128]{1,0:T(8,128)(2,1)S(1)} %copy-done.6), kind=kOutput, calls=%fused_computation.10 | convolution fusion | flops 5373427712 | bytes 82092032 | tf_op jit(solution)/shard_map/td,fd->tf/dot_general | solution.py:36
  287.1 20.1 %fusion.26 = f32[16384,128]{1,0:T(8,128)} fusion(bf16[16384,1184]{0,1:T(8,128)(2,1)} %fusion.3, bf16[128,1184]{0,1:T(8,128)(2,1)S(1)} %copy-done.5), kind=kOutput, calls=%fused_computation.45 | convolution fusion | flops 4966055936 | bytes 47489024 | tf_op jit(solution)/shard_map/tf,df->td/dot_general | solution.py:40
  307.2 0.1 reduce-scatter.8.cloned.1.call-update
  307.3 0.1 reduce-scatter.6.cloned.1.call-start
  307.3 20.2 %fusion.25 = f32[16384,128]{1,0:T(8,128)} fusion(bf16[16384,1184]{0,1:T(8,128)(2,1)} %get-tuple-element.10, bf16[1184,128]{1,0:T(8,128)(2,1)S(1)} %copy-done.6), kind=kOutput, calls=%fused_computation.44 | convolution fusion | flops 4966055936 | bytes 47489024 | tf_op jit(solution)/shard_map/dot_general | solution.py:31
  327.5 0.1 reduce-scatter.6.cloned.1.call-update
  327.6 0.3 all-gather.8.cloned.1.call-start
  327.9 42.0 %reduce-scatter.8.cloned.1.call-done = f32[1024,128]{1,0:T(8,128)} async-done(((f32[16384,128]{1,0:T(8,128)}), f32[1024,128]{1,0:T(8,128)}) %reduce-scatter.8.cloned.1.call-update) | async-done | bytes 524304 | tf_op jit(solution)/shard_map/reduce_scatter | solution.py:41
  369.9 0.0 copy-done.2
  369.9 1.3 fusion.23
  371.2 67.2 %reduce-scatter.6.cloned.1.call-done = f32[1024,128]{1,0:T(8,128)} async-done(((f32[16384,128]{1,0:T(8,128)}), f32[1024,128]{1,0:T(8,128)}) %reduce-scatter.6.cloned.1.call-update) | async-done | bytes 524304 | tf_op jit(solution)/shard_map/reduce_scatter | solution.py:32
  438.4 0.0 copy-done.8
  438.4 2.2 fusion.20
  440.6 0.1 all-gather.8.cloned.1.call-update
  440.7 0.0 copy-start.1
  440.7 19.4 %fusion.27 = f32[1184,128]{1,0:T(8,128)} fusion(bf16[16384,1184]{0,1:T(8,128)(2,1)} %get-tuple-element.10, bf16[16384,128]{1,0:T(8,128)(2,1)} %all-gather.6.cloned.1.call-done), kind=kOutput, calls=%fused_computation.46 | convolution fusion | flops 4966055936 | bytes 43597824 | tf_op jit(solution)/shard_map/tf,td->fd/dot_general | solution.py:38
  460.1 0.0 copy-done.11
  460.1 17.3 %fusion.28 = f32[128,1184]{0,1:T(8,128)} fusion(bf16[16384,1184]{0,1:T(8,128)(2,1)} %fusion.3, bf16[16384,128]{1,0:T(8,128)(2,1)S(1)} %copy-done.11), kind=kOutput, calls=%fused_computation.47 | convolution fusion | flops 4966055936 | bytes 43597824 | tf_op jit(solution)/shard_map/td,tf->df/dot_general | solution.py:39
  477.4 4.0 all-gather.8.cloned.1.call-done
  481.4 90.7 %scatter_custom_fusion = f32[9504,128]{1,0:T(8,128)} fusion(s32[16384]{0:T(1024)} %get-tuple-element.6, bf16[16384,128]{1,0:T(8,128)(2,1)} %all-gather.8.cloned.1.call-done, f32[]{:T(128)} %constant.21.clone.1), kind=kCustom, calls=%fused_computation.18 | custom fusion | flops 4194304 | bytes 9060864 | tf_op jit(solution)/shard_map/scatter-add | solution.py:48
  572.1 0.0 copy-done.1
  (14 shorter events, 0.0 us)
Async XLA Ops:
  7.2 2.6 copy-start
  7.2 74.7 %copy-start.12 = (bf16[128]{0:T(256)(128)(2,1)S(1)}, bf16[128]{0:T(256)(128)(2,1)}, u32[]{:S(2)}) copy-start(bf16[128]{0:T(256)(128)(2,1)} %param.8) | copy-start | bytes 772
  7.2 180.2 %copy-start.4 = (bf16[128,1184]{0,1:T(8,128)(2,1)S(1)}, bf16[128,1184]{0,1:T(8,128)(2,1)}, u32[]{:S(2)}) copy-start(bf16[128,1184]{0,1:T(8,128)(2,1)} %param.9) | copy-start | bytes 909316
  7.2 136.2 %reduce-scatter.4.cloned.1.call-start = ((), (), s32[]{:S(2)}) async-start(), calls=%async_computation.3 | async-start | bytes 4456448 | tf_op jit(solution)/shard_map/reduce_scatter | solution.py:22
  81.8 105.6 %all-gather.4.cloned.1.call-start = ((), (), s32[]{:S(2)}) async-start(), calls=%async_computation.4 | async-start | bytes 4456448 | tf_op jit(solution)/shard_map/all_gather | solution.py:27
  81.9 143.0 %copy-start.9 = (f32[128]{0:T(128)}, f32[128]{0:T(128)S(1)}, u32[]{:S(2)}) copy-start(f32[128]{0:T(128)S(1)} %convert_element_type.34) | copy-start | bytes 1540
  144.6 80.3 %copy-start.7 = (f32[1024]{0:T(1024)}, f32[1024]{0:T(1024)S(1)}, u32[]{:S(2)}) copy-start(f32[1024]{0:T(1024)S(1)} %add_rsqrt_fusion) | copy-start | bytes 12292
  146.6 79.4 %all-gather.6.cloned.1.call-start = ((), (), s32[]{:S(2)}) async-start(), calls=%async_computation.6 | async-start | bytes 4456448 | tf_op jit(solution)/shard_map/all_gather | solution.py:35
  147.4 78.6 %copy-start.6 = (bf16[1184,128]{1,0:T(8,128)(2,1)S(1)}, bf16[1184,128]{1,0:T(8,128)(2,1)}, u32[]{:S(2)}) copy-start(bf16[1184,128]{1,0:T(8,128)(2,1)} %param.10) | copy-start | bytes 909316
  147.4 222.6 %reduce-scatter.8.cloned.1.call-start = ((), (), s32[]{:S(2)}) async-start(), calls=%async_computation.7 | async-start | bytes 8912896 | tf_op jit(solution)/shard_map/reduce_scatter | solution.py:41
  226.0 61.1 %copy-start.5 = (bf16[128,1184]{0,1:T(8,128)(2,1)S(1)}, bf16[128,1184]{0,1:T(8,128)(2,1)}, u32[]{:S(2)}) copy-start(bf16[128,1184]{0,1:T(8,128)(2,1)} %param.9) | copy-start | bytes 909316
  307.2 62.7 %copy-start.2 = (bf16[1024,128]{1,0:T(8,128)(2,1)S(1)}, bf16[1024,128]{1,0:T(8,128)(2,1)}, u32[]{:S(2)}) copy-start(bf16[1024,128]{1,0:T(8,128)(2,1)} %reduce-scatter.4.cloned.1.call-done) | copy-start | bytes 786436
  307.2 62.7 %copy-start.10 = (f32[128]{0:T(128)S(1)}, f32[128]{0:T(128)}, u32[]{:S(2)}) copy-start(f32[128]{0:T(128)} %copy-done.9) | copy-start | bytes 1540
  307.2 131.2 %copy-start.3 = (bf16[1024,128]{1,0:T(8,128)(2,1)S(1)}, bf16[1024,128]{1,0:T(8,128)(2,1)}, u32[]{:S(2)}) copy-start(bf16[1024,128]{1,0:T(8,128)(2,1)} %param.11) | copy-start | bytes 786436
  307.2 131.2 %copy-start.8 = (f32[1024]{0:T(1024)S(1)}, f32[1024]{0:T(1024)}, u32[]{:S(2)}) copy-start(f32[1024]{0:T(1024)} %copy-done.7) | copy-start | bytes 12292
  307.3 131.1 %reduce-scatter.6.cloned.1.call-start = ((), (), s32[]{:S(2)}) async-start(), calls=%async_computation.5 | async-start | bytes 8912896 | tf_op jit(solution)/shard_map/reduce_scatter | solution.py:32
  327.6 153.9 %all-gather.8.cloned.1.call-start = ((), (), s32[]{:S(2)}) async-start(), calls=%async_computation.8 | async-start | bytes 4456448 | tf_op jit(solution)/shard_map/all_gather | solution.py:46
  440.7 19.4 %copy-start.11 = (bf16[16384,128]{1,0:T(8,128)(2,1)S(1)}, bf16[16384,128]{1,0:T(8,128)(2,1)}, u32[]{:S(2)}) copy-start(bf16[16384,128]{1,0:T(8,128)(2,1)} %all-gather.4.cloned.1.call-done) | copy-start | bytes 12582916
  440.7 131.4 %copy-start.1 = (bf16[9504,128]{1,0:T(8,128)(2,1)S(1)}, bf16[9504,128]{1,0:T(8,128)(2,1)}, u32[]{:S(2)}) copy-start(bf16[9504,128]{1,0:T(8,128)(2,1)} %param.7) | copy-start | bytes 7299076
Sparse Core Ops, SparseCore 0:
  81.9 61.5 reduce-scatter.3
  146.7 40.6 all-gather.3
  189.0 36.8 all-gather.5
  307.4 62.4 reduce-scatter.7
  372.1 66.2 reduce-scatter.5
  440.8 40.5 all-gather.7
where the time goes:
time: 580 us; the launch traced here: 579 us
  waiting for transfers between devices  217 us (37%)
  matrix products  176 us (30%)
  other arithmetic  114 us (20%)
  local copies, waits for them, and re-layouts  58.1 us (10%)
  between operations  14.3 us (2%)
    scatter-add x1, other arithmetic, shard_body(): jax.ops.segment_sum(d_embed_all.astype(jnp.float32), scatter_ids, num_seg...  90.7 us
    reduce_scatter x1, waiting for transfers between devices, shard_body(): mlp_out = lax.psum_scatter(mlp_part, 'tp', scatter_dimension=0, tiled=True)  67.2 us
    reduce_scatter x1, waiting for transfers between devices, shard_body(): lax.psum_scatter(lookup_rows, 'tp', scatter_dimension=0, tiled=True)  61.6 us
    dot_general x1, matrix products, shard_body(): jnp.einsum('td,fd->tf', grad_all, w_down, preferred_element_type=jnp.floa...  61.1 us
    gather x1, local copies, waits for them, and re-layouts, shard_body(): lookup_rows = jnp.take(embed_table, safe_ids, axis=0)  58 us
    reduce_scatter x1, waiting for transfers between devices, shard_body(): lax.psum_scatter(d_norm_part, 'tp', scatter_dimension=0, tiled=True)  42 us
    all_gather x1, waiting for transfers between devices, shard_body(): normed_all = lax.all_gather(normed, 'tp', axis=0, tiled=True)  40 us
    dot_general x1, matrix products, shard_body(): jnp.dot(normed_all, w_up, preferred_element_type=jnp.float32)  37.5 us
  transfers between devices with their start and end apart: 6, of which 6 were waited for; matrix products, arithmetic and copies ran while one was open for 17% of the time, Pallas kernels for 0%

commit v1 on v0

v1 whole, which is shorter than its diff:
```python
import functools

import jax
import jax.numpy as jnp
from jax import lax
from jax.experimental import pallas as pl
from jax.experimental.pallas import tpu as pltpu
from jax.sharding import PartitionSpec as P

NORM_EPS = 1e-6
GELU_C = 0.7978845608028654
GELU_A = 0.044715
MESH = pl.DeviceIdType.MESH
F32 = jnp.float32
BF16 = jnp.bfloat16


def remote(src, dst, send_sem, recv_sem, dev):
    return pltpu.make_async_remote_copy(
        src_ref=src, dst_ref=dst, send_sem=send_sem, recv_sem=recv_sem,
        device_id={"tp": dev}, device_id_type=MESH,
    )


def block_kernel(
    chips, sub,
    idx_ref, table_ref, gain_ref, w1_ref, w1t_ref, w2_ref, w2t_ref, dout_ref,
    out_ref, dw1t_ref, dw2_ref, dx_all,
    tab_in, tab_f32, gath, xs, x_t, inv_r, d_all, n_all, h_buf, du_buf, own, psend, precv, rs,
    tab_sem, x_send, x_recv, d_send, d_recv, dp_send, dp_recv, n_send, n_recv, np_send, np_recv,
    e_send, e_recv, ep_send, ep_recv, p_send, p_recv, r_send, r_recv,
):
    me = lax.axis_index("tp")
    chip, core = me // 2, me % 2
    partner = chip * 2 + 1 - core
    up = ((chip + 1) % chips) * 2 + core
    down = ((chip + chips - 1) % chips) * 2 + core
    half_rows = gath.shape[1]
    shard_rows = table_ref.shape[0]
    steps = chips - 1

    def next_dev(half):
        return up * (1 - half) + down * half

    def chip_at(half, hop):
        return (chip + (1 - half) * (chips - hop) + half * hop) % chips

    barrier = pltpu.get_barrier_semaphore()
    for dev in (partner, up, down):
        pl.semaphore_signal(barrier, inc=1, device_id={"tp": dev}, device_id_type=MESH)
    pl.semaphore_wait(barrier, 3)

    def ring_copy(buf, send, recv, half, step):
        blk = chip_at(half, step) * 2 + core
        return remote(buf.at[half, blk], buf.at[half, blk], send.at[half, step], recv.at[half, step], next_dev(half))

    def ring_arrival(buf, send, recv, half, step):
        blk = chip_at(half, step + 1) * 2 + core
        return remote(buf.at[half, blk], buf.at[half, blk], send.at[half, step], recv.at[half, step], next_dev(half))

    def pair_copy(buf, send, recv, half, hop):
        blk = chip_at(half, hop) * 2 + core
        return remote(buf.at[half, blk], buf.at[half, blk], send.at[half, hop], recv.at[half, hop], partner)

    def pair_arrival(buf, send, recv, half, hop):
        blk = chip_at(half, hop) * 2 + 1 - core
        return remote(buf.at[half, blk], buf.at[half, blk], send.at[half, hop], recv.at[half, hop], partner)

    def gather_begin(buf, sems, half):
        send, recv, psend_, precv_ = sems
        ring_copy(buf, send, recv, half, 0).start()
        pair_copy(buf, psend_, precv_, half, 0).start()

    def gather_step(buf, sems, half, step):
        send, recv, psend_, precv_ = sems
        ring_arrival(buf, send, recv, half, step).wait_recv()

        @pl.when(step + 1 < steps)
        def _():
            ring_copy(buf, send, recv, half, step + 1).start()

        pair_copy(buf, psend_, precv_, half, step + 1).start()

    def gather_drain(buf, sems):
        send, recv, psend_, precv_ = sems

        def body(step, _):
            for half in (0, 1):
                ring_copy(buf, send, recv, half, step).wait_send()
            return 0

        lax.fori_loop(0, steps, body, 0)

        def pair_body(hop, _):
            for half in (0, 1):
                pair_copy(buf, psend_, precv_, half, hop).wait_send()
            return 0

        lax.fori_loop(0, chips, pair_body, 0)

    d_sems = (d_send, d_recv, dp_send, dp_recv)
    n_sems = (n_send, n_recv, np_send, np_recv)
    e_sems = (e_send, e_recv, ep_send, ep_recv)

    tab_copy = remote(table_ref, tab_in, tab_sem.at[0], tab_sem.at[1], partner)
    tab_copy.start()
    for half in (0, 1):
        rows = dout_ref[half * half_rows:(half + 1) * half_rows, :].astype(F32)
        d_all[half, me] = rows.T.astype(BF16)
        gather_begin(d_all, d_sems, half)
    dw1t_ref[...] = jnp.zeros(dw1t_ref.shape, F32)
    dw2_ref[...] = jnp.zeros(dw2_ref.shape, F32)
    conv = 32

    def convert(src, start):
        def body(i, _):
            at = pl.multiple_of(i * conv, conv)
            dst = pl.multiple_of(start + i * conv, conv)
            tab_f32[pl.ds(dst, conv), :] = src[pl.ds(at, conv), :].astype(F32)
            return 0

        lax.fori_loop(0, shard_rows // conv, body, 0)

    convert(table_ref, core * shard_rows)
    tab_f32[pl.ds(2 * shard_rows, 8), :] = jnp.zeros((8, tab_f32.shape[1]), F32)
    tab_copy.wait()
    convert(tab_in, (1 - core) * shard_rows)

    def x_copy(half, step):
        return remote(xs.at[half, step], xs.at[half, step + 1], x_send.at[half, step], x_recv.at[half, step],
                      next_dev(half))

    unroll = 8

    def look_step(step, _):
        for half in (0, 1):
            base = (chip_at(half, step + 1) * 2 + half) * half_rows

            def rows_body(i, _):
                at = i * unroll
                for j in range(unroll):
                    row = idx_ref[base + at + j]
                    gath[half, pl.ds(at + j, 1), :] = tab_f32[pl.ds(row, 1), :]
                return 0

            lax.fori_loop(0, half_rows // unroll, rows_body, 0)

            @pl.when(step == 0)
            def _():
                xs[half, step] = gath[half].astype(BF16)

            @pl.when(step > 0)
            def _():
                x_copy(half, step - 1).wait_recv()
                xs[half, step] = (gath[half] + xs[half, step].astype(F32)).astype(BF16)

            @pl.when(step < steps)
            def _():
                x_copy(half, step).start()

        @pl.when(step < steps)
        def _():
            for half in (0, 1):
                gather_step(d_all, d_sems, half, step)

        return 0

    lax.fori_loop(0, chips, look_step, 0)

    gain = gain_ref[...]
    for half in (0, 1):
        rows_t = xs[half, steps].astype(F32).T
        inv = lax.rsqrt(jnp.mean(rows_t * rows_t, axis=0, keepdims=True) + NORM_EPS)
        x_t[half] = rows_t
        inv_r[half] = inv
        n_all[half, me] = (rows_t * inv * gain).astype(BF16)
        gather_begin(n_all, n_sems, half)

    def d_wait(hop, _):
        for half in (0, 1):
            pair_arrival(d_all, dp_send, dp_recv, half, hop).wait_recv()
        return 0

    lax.fori_loop(0, chips, d_wait, 0)

    def mlp(half, blk, dst):
        def body(i, _):
            cols = pl.ds(pl.multiple_of(i * sub, sub), sub)
            n_t = n_all[half, blk, :, cols]
            d_t = d_all[half, blk, :, cols]
            u = jnp.dot(w1t_ref[...], n_t, preferred_element_type=F32).astype(BF16).astype(F32)
            dh = jnp.dot(w2_ref[...], d_t, preferred_element_type=F32)
            sq = u * u
            th = jnp.tanh(u * (GELU_C + (GELU_C * GELU_A) * sq))
            sg = 0.5 + 0.5 * th
            h = u * sg
            slope = sg + (h * (1.0 - sg)) * (2.0 * GELU_C + (6.0 * GELU_C * GELU_A) * sq)
            h = h.astype(BF16)
            du = (dh * slope).astype(BF16)
            h_buf[...] = h
            du_buf[...] = du
            h = h_buf[...]
            du = du_buf[...]
            dst[0, :, cols] = jnp.dot(w2t_ref[...], h, preferred_element_type=F32)
            dst[1, :, cols] = jnp.dot(w1_ref[...], du, preferred_element_type=F32)
            nt = (((1,), (1,)), ((), ()))
            dw2_ref[...] += lax.dot_general(h, d_t, nt, preferred_element_type=F32)
            dw1t_ref[...] += lax.dot_general(du, n_t, nt, preferred_element_type=F32)
            return 0

        lax.fori_loop(0, half_rows // sub, body, 0)

    def p_copy(half, step):
        return remote(psend.at[step % 2, half], precv.at[step, half], p_send.at[step, half], p_recv.at[step, half],
                      partner)

    def r_copy(half, val, step):
        return remote(rs.at[step, half, val], rs.at[step + 1, half, val], r_send.at[step, half, val],
                      r_recv.at[step, half, val], next_dev(half))

    for half in (0, 1):
        gather_step(n_all, n_sems, half, 0)

    def sum_step(step, _):
        hop = (step + 1) % chips

        def part(i, _):
            half, mine = i % 2, i // 2
            blk = chip_at(half, hop) * 2 + (1 - core) * (1 - mine) + core * mine

            @pl.when(mine == 0)
            def _():
                pair_arrival(n_all, np_send, np_recv, half, hop).wait_recv()

                @pl.when(step >= 2)
                def _():
                    p_copy(half, step - 2).wait_send()

            @pl.when((i == 2) & (step + 1 < steps))
            def _():
                for h in (0, 1):
                    gather_step(n_all, n_sems, h, step + 1)

            mlp(half, blk, own.at[i])

            @pl.when(mine == 0)
            def _():
                psend[step % 2, half] = own[i]
                p_copy(half, step).start()

            @pl.when(mine == 1)
            def _():
                p_copy(half, step).wait_recv()
                for val in (0, 1):
                    @pl.when(step == 0)
                    def _():
                        rs[step, half, val] = own[i, val] + precv[step, half, val]

                    @pl.when(step > 0)
                    def _():
                        r_copy(half, val, step - 1).wait_recv()
                        rs[step, half, val] = rs[step, half, val] + (own[i, val] + precv[step, half, val])

                    @pl.when(step < steps)
                    def _():
                        r_copy(half, val, step).start()

            return 0

        lax.fori_loop(0, 4, part, 0)
        return 0

    lax.fori_loop(0, chips, sum_step, 0)

    for half in (0, 1):
        xv = x_t[half]
        inv = inv_r[half]
        rows = slice(half * half_rows, (half + 1) * half_rows)
        scaled = rs[steps, half, 1] * gain
        mean = jnp.mean(xv * scaled, axis=0, keepdims=True)
        dx = inv * (scaled - xv * inv * inv * mean)
        dx = dout_ref[rows, :].astype(F32) + dx.T
        dx_all[half, me] = dx.astype(BF16)
        gather_begin(dx_all, e_sems, half)
    for half in (0, 1):
        rows = slice(half * half_rows, (half + 1) * half_rows)
        out_ref[rows, :] = (x_t[half] + rs[steps, half, 0]).T.astype(BF16)

    def e_step(step, _):
        for half in (0, 1):
            gather_step(dx_all, e_sems, half, step)
        return 0

    lax.fori_loop(0, steps, e_step, 0)

    def e_wait(hop, _):
        for half in (0, 1):
            pair_arrival(dx_all, ep_send, ep_recv, half, hop).wait_recv()
        return 0

    lax.fori_loop(0, chips, e_wait, 0)

    for buf, sems in ((d_all, d_sems), (n_all, n_sems), (dx_all, e_sems)):
        gather_drain(buf, sems)

    def drain(step, _):
        for half in (0, 1):
            x_copy(half, step).wait_send()
            for val in (0, 1):
                r_copy(half, val, step).wait_send()
        return 0

    lax.fori_loop(0, steps, drain, 0)
    for half in (0, 1):
        for step in (chips - 2, chips - 1):
            p_copy(half, step).wait_send()


def run_block(chips, idx, table, gain, w_up, w_down, d_out):
    rows, dim = d_out.shape
    shard_rows = table.shape[0]
    hidden = w_down.shape[0]
    half = rows // 2
    devs = 2 * chips
    sub = min(256, half)
    dma = pltpu.SemaphoreType.DMA
    vmem = pl.BlockSpec(memory_space=pltpu.VMEM)
    w_up_t, w_down_t = w_up.T, w_down.T
    tokens = rows * devs
    return pl.pallas_call(
        functools.partial(block_kernel, chips, sub),
        out_shape=(
            jax.ShapeDtypeStruct((rows, dim), BF16),
            jax.ShapeDtypeStruct((hidden, dim), F32),
            jax.ShapeDtypeStruct((hidden, dim), F32),
            jax.ShapeDtypeStruct((2, devs, half, dim), BF16),
        ),
        in_specs=[pl.BlockSpec(memory_space=pltpu.SMEM)] + [vmem] * 7,
        out_specs=(vmem,) * 4,
        scratch_shapes=[
            pltpu.VMEM((shard_rows, dim), BF16),
            pltpu.VMEM((2 * shard_rows + 8, dim), F32),
            pltpu.VMEM((2, half, dim), F32),
            pltpu.VMEM((2, chips, half, dim), BF16),
            pltpu.VMEM((2, dim, half), F32),
            pltpu.VMEM((2, 1, half), F32),
            pltpu.VMEM((2, devs, dim, half), BF16),
            pltpu.VMEM((2, devs, dim, half), BF16),
            pltpu.VMEM((hidden, sub), BF16),
            pltpu.VMEM((hidden, sub), BF16),
            pltpu.VMEM((4, 2, dim, half), F32),
            pltpu.VMEM((2, 2, 2, dim, half), F32),
            pltpu.VMEM((chips, 2, 2, dim, half), F32),
            pltpu.VMEM((chips, 2, 2, dim, half), F32),
            dma((2,)),
            dma((2, chips - 1)), dma((2, chips - 1)),
            dma((2, chips - 1)), dma((2, chips - 1)), dma((2, chips)), dma((2, chips)),
            dma((2, chips - 1)), dma((2, chips - 1)), dma((2, chips)), dma((2, chips)),
            dma((2, chips - 1)), dma((2, chips - 1)), dma((2, chips)), dma((2, chips)),
            dma((chips, 2)), dma((chips, 2)),
            dma((chips - 1, 2, 2)), dma((chips - 1, 2, 2)),
        ],
        compiler_params=pltpu.CompilerParams(
            collective_id=0, has_side_effects=True, vmem_limit_bytes=67043328,
        ),
        cost_estimate=pl.CostEstimate(flops=12 * tokens * hidden * dim, bytes_accessed=tokens * dim * 8,
                                      transcendentals=0),
        name="block",
    )(idx, table, gain, w_up, w_up_t, w_down, w_down_t, d_out)


def scatter_kernel(rel_ref, words_ref, dx_ref, grad_ref, dx_f32):
    grad_ref[...] = jnp.zeros(grad_ref.shape, F32)
    conv = 128

    def convert(i, _):
        at = pl.multiple_of(i * conv, conv)
        dx_f32[pl.ds(at, conv), :] = dx_ref[pl.ds(at, conv), :].astype(F32)
        return 0

    lax.fori_loop(0, dx_ref.shape[0] // conv, convert, 0)

    def word_body(w, _):
        def cond(bits):
            return bits != 0

        def step(bits):
            low = bits & (-bits)
            tok = w * 32 + 31 - lax.clz(low)
            row = rel_ref[tok]
            grad_ref[pl.ds(row, 1), :] += dx_f32[pl.ds(tok, 1), :]
            return bits & (bits - 1)

        lax.while_loop(cond, step, words_ref[w])
        return 0

    lax.fori_loop(0, words_ref.shape[0], word_body, 0)


def scatter_rows(ids, base, shard_rows, dx_all):
    tokens, dim = dx_all.shape
    rel = ids - base
    owned = (rel >= 0) & (rel < shard_rows)
    bit = jnp.left_shift(jnp.int32(1), lax.broadcasted_iota(jnp.int32, (tokens // 32, 32), 1))
    words = jnp.sum(jnp.where(owned.reshape(tokens // 32, 32), bit, 0), axis=1, dtype=jnp.int32)
    smem = pl.BlockSpec(memory_space=pltpu.SMEM)
    vmem = pl.BlockSpec(memory_space=pltpu.VMEM)
    return pl.pallas_call(
        scatter_kernel,
        out_shape=jax.ShapeDtypeStruct((shard_rows, dim), F32),
        in_specs=[smem, smem, vmem],
        out_specs=vmem,
        scratch_shapes=[pltpu.VMEM((tokens, dim), F32)],
        compiler_params=pltpu.CompilerParams(vmem_limit_bytes=40 * 1024 * 1024),
        name="scatter",
    )(rel, words, dx_all)


def solution(mesh):
    chips = mesh.shape["tp"] // 2

    def shard_body(token_ids, embed_table, norm_gain, w_up, w_down, d_out):
        shard_rows, dim = embed_table.shape
        rows = d_out.shape[0]
        me = lax.axis_index("tp")
        chip, core = me // 2, me % 2
        rel = token_ids - chip * (2 * shard_rows)
        idx = jnp.where((rel >= 0) & (rel < 2 * shard_rows), rel, 2 * shard_rows)
        idx = lax.dynamic_index_in_dim(idx.reshape(chips, 2, rows), core, 1, keepdims=False).reshape(-1)
        gain = jnp.broadcast_to(norm_gain.astype(F32)[:, None], (dim, rows // 2))
        block_out, dw1t, dw2, dx_all = run_block(chips, idx, embed_table, gain, w_up, w_down, d_out)
        ids = token_ids.reshape(2 * chips, 2, rows // 2).transpose(1, 0, 2).reshape(-1)
        grad_table = scatter_rows(ids, me * shard_rows, shard_rows, dx_all.reshape(-1, dim))
        return block_out, grad_table, dw1t.T, dw2

    return jax.shard_map(
        shard_body,
        mesh=mesh,
        in_specs=(P("dp"), P("tp", None), P(), P(None, "tp"), P("tp", None), P(("dp", "tp"), None)),
        out_specs=(P(("dp", "tp"), None), P(("dp", "tp"), None), P("dp", "tp"), P(("dp", "tp"), None)),
        check_vma=False,
    )
```

time: 580 us -> 246 us (0.42)
  Pallas kernels: 0 us -> 230 us
  waiting for transfers between devices: 217 us -> 0 us
  matrix products: 176 us -> 0 us
  other arithmetic: 114 us -> 2.46 us
  local copies, waits for them, and re-layouts: 58.1 us -> 12.8 us
  between operations: 14.3 us -> 0.74 us
    pallas_call x0 -> x2, Pallas kernels: none -> 230 us  [the longest x1 210 us: run_block(): pl.pallas_call(functools.partial(block_kernel, chips, sub), out_shape=(ja...]
    dot_general x6 -> x0, matrix products: 176 us -> none  [the longest x1 61.1 us: shard_body(): jnp.einsum('td,fd->tf', grad_all, w_down, preferred_element_type=jnp.floa...]
    reduce_scatter x3 -> x0, waiting for transfers between devices: 171 us -> none  [the longest x1 67.2 us: shard_body(): mlp_out = lax.psum_scatter(mlp_part, 'tp', scatter_dimension=0, tiled=True)]
    scatter-add x1 -> x0, other arithmetic: 90.7 us -> none  [shard_body(): jax.ops.segment_sum(d_embed_all.astype(jnp.float32), scatter_ids, num_seg...]
    gather x1 -> x0, local copies, waits for them, and re-layouts: 58 us -> none  [shard_body(): lookup_rows = jnp.take(embed_table, safe_ids, axis=0)]
    all_gather x3 -> x0, waiting for transfers between devices: 45.1 us -> none  [the longest x1 40 us: shard_body(): normed_all = lax.all_gather(normed, 'tp', axis=0, tiled=True)]
    select_n x2 -> x1, other arithmetic: 15.4 us -> 0.86 us  [shard_body(): idx = jnp.where((rel >= 0) & (rel < 2 * shard_rows), rel, 2 * shard_rows)]
    unnamed x26 -> x18, local copies, waits for them, and re-layouts: 0.07 us -> 10.4 us
  transfers between devices with their start and end apart: 6 -> 0, of which waited for: 6 -> 0; matrix products, arithmetic and copies ran while one was open for 17% -> 0% of each run, Pallas kernels for 0% -> 0%
where the time goes in v1:
time: 246 us
  Pallas kernels  230 us (93%)
  local copies, waits for them, and re-layouts  12.8 us (5%)
  other arithmetic  2.46 us (1%)
    pallas_call x1, Pallas kernels, run_block(): pl.pallas_call(functools.partial(block_kernel, chips, sub), out_shape=(ja...  210 us
    pallas_call x1, Pallas kernels, scatter_rows(): pl.pallas_call(scatter_kernel, out_shape=jax.ShapeDtypeStruct((shard_rows...  20 us
    unnamed x18, local copies, waits for them, and re-layouts  10.4 us

profile of v1, /device:TPU:21, one launch (start us, length us, event | category | flops | bytes accessed | tf_op | source)
XLA Modules:
  0.0 245.6 jit_solution(2814143366114948240)
XLA Ops:
  0.7 0.9 and_select_fusion
  1.6 0.6 constant_dynamic-slice_fusion
  2.2 0.9 compare_and_fusion
  3.1 0.2 and.29
  3.3 0.7 select_reduce_fusion.words_ref
  4.1 0.6 copy.19
  4.7 1.4 broadcast_in_dim.5.gain_ref
  6.2 1.9 copy.16.w1_ref
  8.0 1.9 copy.15
  9.9 209.6 %block.1 = (bf16[1024,128]{1,0:T(8,128)(2,1)}, f32[1184,128]{1,0:T(8,128)}, f32[1184,128]{1,0:T(8,128)}, bf16[2,16,512,128]{3,2,1,0:T(8,128)(2,1)}) custom-call(s32[8192]{0:T(1024)} %bitcast.17, bf16[9504,128]{1,0:T(8,128)(2,1)} %table_ref.1, f32[128,512]{1,0:T(8,128)} %broadcast_in_dim.5.gain_ref, bf16[128,1184]{1,0:T(8,128)(2,1)} %copy.16.w1_ref, ...), custom_call_target="tpu_custom_call" | custom-call | flops 29796335616 | bytes 16777216 | tf_op jit(solution)/shard_map/block/pallas_call | solution.py:330
  219.5 0.0 copy-start
  219.5 2.2 copy-done
  221.7 0.0 copy-start.1
  221.7 0.8 copy-done.1
  222.5 0.0 copy-start.2
  222.5 0.7 copy-done.2
  223.2 0.0 copy-start.5
  223.2 0.0 copy-start.4
  223.2 0.0 copy-start.3
  223.2 20.0 %scatter.1 = f32[9504,128]{1,0:T(8,128)} custom-call(s32[16384]{0:T(1024)S(1)} %bitcast.10, s32[512]{0:T(512)S(1)} %copy-done.2, bf16[16384,128]{1,0:T(8,128)(2,1)S(1)} %bitcast.9), custom_call_target="tpu_custom_call" | custom-call | tf_op jit(solution)/shard_map/scatter/pallas_call | solution.py:408
  243.2 0.0 copy-done.5
  243.2 0.7 copy.23
  243.9 0.0 copy-done.4
  243.9 0.8 copy.24
  244.7 0.0 copy-done.3
  244.7 0.8 copy.25
  (6 shorter events, 0.1 us)
Async XLA Ops:
  219.5 2.2 copy-start
  221.7 0.8 copy-start.1
  222.5 0.7 copy-start.2
  223.2 20.0 %copy-start.5 = (bf16[1024,128]{1,0:T(8,128)(2,1)S(1)}, bf16[1024,128]{1,0:T(8,128)(2,1)}, u32[]{:S(2)}) copy-start(bf16[1024,128]{1,0:T(8,128)(2,1)} %get-tuple-element.18) | copy-start | bytes 786436
  223.2 20.7 %copy-start.4 = (f32[1184,128]{1,0:T(8,128)S(1)}, f32[1184,128]{1,0:T(8,128)}, u32[]{:S(2)}) copy-start(f32[1184,128]{1,0:T(8,128)} %get-tuple-element.10) | copy-start | bytes 1818628
  223.2 21.6 %copy-start.3 = (f32[1184,128]{1,0:T(8,128)S(1)}, f32[1184,128]{1,0:T(8,128)}, u32[]{:S(2)}) copy-start(f32[1184,128]{1,0:T(8,128)} %get-tuple-element.21) | copy-start | bytes 1818628

commit v2 on v1

v2 whole, which is shorter than its diff:
```python
import functools

import jax
import jax.numpy as jnp
from jax import lax
from jax.experimental import pallas as pl
from jax.experimental.pallas import tpu as pltpu
from jax.sharding import PartitionSpec as P

NORM_EPS = 1e-6
GELU_C = 0.7978845608028654
GELU_A = 0.044715
MESH = pl.DeviceIdType.MESH
F32 = jnp.float32
BF16 = jnp.bfloat16


def remote(src, dst, send_sem, recv_sem, dev):
    return pltpu.make_async_remote_copy(
        src_ref=src, dst_ref=dst, send_sem=send_sem, recv_sem=recv_sem,
        device_id={"tp": dev}, device_id_type=MESH,
    )


def block_kernel(
    chips, sub, tiles,
    ids_ref, ids_vec, table_ref, gain_ref, w1t_ref, w2_ref, dout_ref,
    out_ref, dw1t_ref, dw2_ref, dx_all, list_ref, count_ref,
    tab_in, tab_f32, gath, xs, x_t, inv_r, gain_t, w1_ref, w2t_ref, d_all, n_all, h_buf, du_buf, parts, precv, rs,
    tab_sem, x_send, x_recv, d_send, d_recv, dp_send, dp_recv, n_send, n_recv, np_send, np_recv,
    e_send, e_recv, ep_send, ep_recv, p_send, p_recv, r_send, r_recv,
):
    me = lax.axis_index("tp")
    chip, core = me // 2, me % 2
    partner = chip * 2 + 1 - core
    up = ((chip + 1) % chips) * 2 + core
    down = ((chip + chips - 1) % chips) * 2 + core
    half_rows, dim = gath.shape[1:]
    shard_rows = table_ref.shape[0]
    steps = chips - 1

    def next_dev(half):
        return up * (1 - half) + down * half

    def chip_at(half, hop):
        return (chip + (1 - half) * (chips - hop) + half * hop) % chips

    barrier = pltpu.get_barrier_semaphore()
    for dev in (partner, up, down):
        pl.semaphore_signal(barrier, inc=1, device_id={"tp": dev}, device_id_type=MESH)
    pl.semaphore_wait(barrier, 3)

    def ring_copy(buf, send, recv, half, hop, step, piece):
        blk = chip_at(half, hop) * 2 + core
        pieces = send.shape[2]
        size = buf.shape[2] // pieces
        ref = buf.at[half, blk, pl.ds(piece * size, size)]
        return remote(ref, ref, send.at[half, step, piece], recv.at[half, step, piece], next_dev(half))

    def pair_copy(buf, send, recv, half, hop):
        blk = chip_at(half, hop) * 2 + core
        return remote(buf.at[half, blk], buf.at[half, blk], send.at[half, hop], recv.at[half, hop], partner)

    def pair_arrival(buf, send, recv, half, hop):
        blk = chip_at(half, hop) * 2 + 1 - core
        return remote(buf.at[half, blk], buf.at[half, blk], send.at[half, hop], recv.at[half, hop], partner)

    def gather_begin(buf, sems, half):
        send, recv, psend_, precv_ = sems
        for piece in range(send.shape[2]):
            ring_copy(buf, send, recv, half, 0, 0, piece).start()
        pair_copy(buf, psend_, precv_, half, 0).start()

    def gather_step(buf, sems, step):
        send, recv, psend_, precv_ = sems
        for piece in range(send.shape[2]):
            for half in (0, 1):
                ring_copy(buf, send, recv, half, step + 1, step, piece).wait_recv()

                @pl.when(step + 1 < steps)
                def _():
                    ring_copy(buf, send, recv, half, step + 1, step + 1, piece).start()

        for half in (0, 1):
            pair_copy(buf, psend_, precv_, half, step + 1).start()

    def gather_drain(buf, sems):
        send, recv, psend_, precv_ = sems

        def body(step, _):
            for half in (0, 1):
                for piece in range(send.shape[2]):
                    ring_copy(buf, send, recv, half, step, step, piece).wait_send()
            return 0

        lax.fori_loop(0, steps, body, 0)

        def pair_body(hop, _):
            for half in (0, 1):
                pair_copy(buf, psend_, precv_, half, hop).wait_send()
            return 0

        lax.fori_loop(0, chips, pair_body, 0)

    d_sems = (d_send, d_recv, dp_send, dp_recv)
    n_sems = (n_send, n_recv, np_send, np_recv)
    e_sems = (e_send, e_recv, ep_send, ep_recv)

    tab_copy = remote(table_ref, tab_in, tab_sem.at[0], tab_sem.at[1], partner)
    tab_copy.start()
    for half in (0, 1):
        rows = dout_ref[half * half_rows:(half + 1) * half_rows, :].astype(F32)
        d_all[half, me] = rows.T.astype(BF16)
        gather_begin(d_all, d_sems, half)
    conv = 32

    def convert(src, start):
        def body(i, _):
            at = pl.multiple_of(i * conv, conv)
            dst = pl.multiple_of(start + i * conv, conv)
            tab_f32[pl.ds(dst, conv), :] = src[pl.ds(at, conv), :].astype(F32)
            return 0

        lax.fori_loop(0, shard_rows // conv, body, 0)

    convert(table_ref, core * shard_rows)
    tab_f32[pl.ds(2 * shard_rows, 8), :] = jnp.zeros((8, dim), F32)
    tab_copy.wait()
    convert(tab_in, (1 - core) * shard_rows)

    pieces = x_send.shape[2]
    size = half_rows // pieces

    def x_copy(half, step, piece):
        rows = pl.ds(piece * size, size)
        return remote(xs.at[half, step, rows], xs.at[half, step + 1, rows], x_send.at[half, step, piece],
                      x_recv.at[half, step, piece], next_dev(half))

    unroll = 8
    chip_base = chip * (2 * shard_rows)
    none = jnp.uint32(2 * shard_rows)

    def look_step(step, _):
        for half in (0, 1):
            base = ((chip_at(half, step + 1) * 2 + core) * 2 + half) * half_rows

            def rows_body(i, _):
                at = i * unroll
                for j in range(unroll):
                    row = (ids_ref[base + at + j] - chip_base).astype(jnp.uint32)
                    row = jnp.minimum(row, none).astype(jnp.int32)
                    gath[half, pl.ds(at + j, 1), :] = tab_f32[pl.ds(row, 1), :]
                return 0

            lax.fori_loop(0, half_rows // unroll, rows_body, 0)

        for piece in range(pieces):
            rows = slice(piece * size, (piece + 1) * size)
            for half in (0, 1):
                @pl.when(step == 0)
                def _():
                    xs[half, step, rows] = gath[half, rows].astype(BF16)

                @pl.when(step > 0)
                def _():
                    x_copy(half, step - 1, piece).wait_recv()
                    xs[half, step, rows] = (gath[half, rows] + xs[half, step, rows].astype(F32)).astype(BF16)

                @pl.when(step < steps)
                def _():
                    x_copy(half, step, piece).start()

        @pl.when(step < steps)
        def _():
            gather_step(d_all, d_sems, step)

        @pl.when(step == 0)
        def _():
            setup()

        @pl.when(step > 0)
        def _():
            owned_lists(step)

        return 0

    def setup():
        dw1t_ref[...] = jnp.zeros(dw1t_ref.shape, F32)
        dw2_ref[...] = jnp.zeros(dw2_ref.shape, F32)
        w1_ref[...] = w1t_ref[...].astype(F32).T.astype(BF16)
        w2t_ref[...] = w2_ref[...].astype(F32).T.astype(BF16)
        gain_t[...] = jnp.broadcast_to(gain_ref[...].astype(F32), (dim, dim)).T
        rel = ids_vec[...] - me * shard_rows
        owned = ((rel >= 0) & (rel < shard_rows)).astype(F32).astype(BF16)
        nt = (((1,), (1,)), ((), ()))
        ones = jnp.ones((8, ids_vec.shape[1]), BF16)
        count_ref[...] = lax.dot_general(ones, owned, nt, preferred_element_type=F32).astype(jnp.int32)

    groups = ids_vec.shape[0]
    width = ids_vec.shape[1]
    batch = 8
    turns = groups // batch
    per_step = -(-turns // steps)

    def owned_lists(step):
        lane = lax.broadcasted_iota(jnp.int32, (batch, width), 1)
        sub8 = lax.broadcasted_iota(jnp.int32, (8, width), 0)
        before = (lax.broadcasted_iota(jnp.int32, (width, width), 0)
                  < lax.broadcasted_iota(jnp.int32, (width, width), 1)).astype(F32).astype(BF16)
        place = lax.broadcasted_iota(jnp.int32, (width, width), 0)
        nt = (((1,), (1,)), ((), ()))

        def turn(t, _):
            at = pl.multiple_of(t * batch, batch)
            rel = ids_vec[pl.ds(at, batch), :] - me * shard_rows
            owned = (rel >= 0) & (rel < shard_rows)
            rank = jnp.dot(owned.astype(F32).astype(BF16), before, preferred_element_type=F32).astype(jnp.int32)
            rank = jnp.where(owned, rank, -1)
            rel = jnp.where(owned, rel, 0)
            lines = []
            for g in range(batch):
                hot = (jnp.broadcast_to(rank[g:g + 1], (width, width)) == place).astype(F32).astype(BF16)
                row = jnp.broadcast_to(rel[g:g + 1], (8, width))
                vals = jnp.where(sub8 == 0, lane[:8], jnp.where(sub8 == 1, row // width, row % width))
                got = lax.dot_general(vals.astype(F32).astype(BF16), hot, nt, preferred_element_type=F32)
                got = got.astype(jnp.int32)
                lines.append((got[1:2] * width + got[2:3]) * width + got[0:1])
            list_ref[pl.ds(at, batch), :] = jnp.concatenate(lines, axis=0)
            return 0

        first = jnp.minimum((step - 1) * per_step, turns)
        last = jnp.minimum(step * per_step, turns)
        lax.fori_loop(first, last, turn, 0)

    lax.fori_loop(0, chips, look_step, 0)

    gain = jnp.concatenate([gain_t[...]] * (half_rows // dim), axis=1)
    for half in (0, 1):
        rows_t = xs[half, steps].astype(F32).T
        inv = lax.rsqrt(jnp.mean(rows_t * rows_t, axis=0, keepdims=True) + NORM_EPS)
        x_t[half] = rows_t
        inv_r[half] = inv
        n_all[half, me] = (rows_t * inv * gain).astype(BF16)
        gather_begin(n_all, n_sems, half)

    def d_wait(hop, _):
        for half in (0, 1):
            pair_arrival(d_all, dp_send, dp_recv, half, hop).wait_recv()
        return 0

    lax.fori_loop(0, chips, d_wait, 0)

    nt = (((1,), (1,)), ((), ()))

    def mlp(half, blk, dst):
        def body(i, _):
            cols = pl.ds(pl.multiple_of(i * sub, sub), sub)
            n_t = n_all[half, blk, :, cols]
            d_t = d_all[half, blk, :, cols]
            for lo, hi in tiles:
                u = jnp.dot(w1t_ref[lo:hi], n_t, preferred_element_type=F32).astype(BF16).astype(F32)
                dh = jnp.dot(w2_ref[lo:hi], d_t, preferred_element_type=F32)
                sq = (GELU_C * GELU_A) * (u * u)
                th = jnp.tanh(u * (GELU_C + sq))
                sg = 0.5 + 0.5 * th
                h = u * sg
                slope = sg + (h * (1.0 - th)) * (GELU_C + 3.0 * sq)
                h_buf[lo:hi] = h.astype(BF16)
                du_buf[lo:hi] = (dh * slope).astype(BF16)
            h = h_buf[...]
            du = du_buf[...]
            dst[0, :, cols] = jnp.dot(w2t_ref[...], h, preferred_element_type=F32)
            dst[1, :, cols] = jnp.dot(w1_ref[...], du, preferred_element_type=F32)
            dw2_ref[...] += lax.dot_general(h, d_t, nt, preferred_element_type=F32)
            dw1t_ref[...] += lax.dot_general(du, n_t, nt, preferred_element_type=F32)
            return 0

        lax.fori_loop(0, half_rows // sub, body, 0)

    def p_copy(half, hop):
        return remote(parts.at[(hop % 2) * 2 + half], precv.at[hop, half], p_send.at[hop, half], p_recv.at[hop, half],
                      partner)

    def r_copy(half, val, step):
        return remote(rs.at[step, half, val], rs.at[step + 1, half, val], r_send.at[step, half, val],
                      r_recv.at[step, half, val], next_dev(half))

    def part(g, _):
        early = jnp.where(g < 2, 1, 0)
        turn = jnp.maximum(g - 2, 0)
        step = jnp.where(g < 2, steps, turn // 4)
        late = jnp.where((g >= 2) & (step == steps), 1, 0)
        mine = jnp.where(g < 2, 0, jnp.maximum((turn % 4) // 2, late))
        half = g % 2
        hop = (step + 1) % chips
        blk = chip_at(half, hop) * 2 + (1 - core) * (1 - mine) + core * mine

        ahead = turn // 2
        @pl.when((early == 0) & (half == 0) & (ahead < steps))
        def _():
            gather_step(n_all, n_sems, ahead)

        @pl.when(mine == 0)
        def _():
            pair_arrival(n_all, np_send, np_recv, half, hop).wait_recv()

            @pl.when(hop >= 2)
            def _():
                p_copy(half, hop - 2).wait_send()

        spot = jnp.where(mine == 0, (hop % 2) * 2 + half, 4)
        mlp(half, blk, parts.at[spot])

        @pl.when(mine == 0)
        def _():
            p_copy(half, hop).start()

        @pl.when(mine == 1)
        def _():
            p_copy(half, hop).wait_recv()
            for val in (0, 1):
                @pl.when(step == 0)
                def _():
                    rs[step, half, val] = parts[4, val] + precv[hop, half, val]

                @pl.when(step > 0)
                def _():
                    r_copy(half, val, step - 1).wait_recv()
                    rs[step, half, val] = rs[step, half, val] + (parts[4, val] + precv[hop, half, val])

                @pl.when(step < steps)
                def _():
                    r_copy(half, val, step).start()

        return 0

    lax.fori_loop(0, 4 * chips, part, 0)

    gain = jnp.concatenate([gain_t[...]] * (half_rows // dim), axis=1)
    for half in (0, 1):
        xv = x_t[half]
        inv = inv_r[half]
        rows = slice(half * half_rows, (half + 1) * half_rows)
        scaled = rs[steps, half, 1] * gain
        mean = jnp.mean(xv * scaled, axis=0, keepdims=True)
        dx = inv * (scaled - xv * inv * inv * mean)
        dx = dout_ref[rows, :].astype(F32) + dx.T
        dx_all[half, me] = dx.astype(BF16)
        gather_begin(dx_all, e_sems, half)
    for half in (0, 1):
        rows = slice(half * half_rows, (half + 1) * half_rows)
        out_ref[rows, :] = (x_t[half] + rs[steps, half, 0]).T.astype(BF16)

    def e_step(step, _):
        gather_step(dx_all, e_sems, step)
        return 0

    lax.fori_loop(0, steps, e_step, 0)

    for buf, sems in ((d_all, d_sems), (n_all, n_sems)):
        gather_drain(buf, sems)

    def drain(step, _):
        for half in (0, 1):
            for piece in range(pieces):
                x_copy(half, step, piece).wait_send()
            for val in (0, 1):
                r_copy(half, val, step).wait_send()
        return 0

    lax.fori_loop(0, steps, drain, 0)
    for half in (0, 1):
        for hop in (chips - 2, chips - 1):
            p_copy(half, hop).wait_send()
    gather_drain(dx_all, e_sems)

    def e_wait(hop, _):
        for half in (0, 1):
            pair_arrival(dx_all, ep_send, ep_recv, half, hop).wait_recv()
        return 0

    lax.fori_loop(0, chips, e_wait, 0)


def row_tiles(hidden):
    if hidden < 256:
        return ((0, hidden),)
    cut = (hidden // 2) // 16 * 16
    return ((0, cut), (cut, hidden))


def run_block(chips, ids, table, gain, w_up, w_down, d_out):
    rows, dim = d_out.shape
    shard_rows = table.shape[0]
    hidden = w_down.shape[0]
    half = rows // 2
    devs = 2 * chips
    sub = min(256, half)
    dma = pltpu.SemaphoreType.DMA
    vmem = pl.BlockSpec(memory_space=pltpu.VMEM)
    tokens = rows * devs
    groups = tokens // dim

    def gather_sems(pieces):
        ring, pair = (2, chips - 1, pieces), (2, chips)
        return [dma(ring), dma(ring), dma(pair), dma(pair)]

    return pl.pallas_call(
        functools.partial(block_kernel, chips, sub, row_tiles(hidden)),
        out_shape=(
            jax.ShapeDtypeStruct((rows, dim), BF16),
            jax.ShapeDtypeStruct((hidden, dim), F32),
            jax.ShapeDtypeStruct((hidden, dim), F32),
            jax.ShapeDtypeStruct((2, devs, half, dim), BF16),
            jax.ShapeDtypeStruct((groups, dim), jnp.int32),
            jax.ShapeDtypeStruct((8, groups), jnp.int32),
        ),
        in_specs=[pl.BlockSpec(memory_space=pltpu.SMEM)] + [vmem] * 6,
        out_specs=(vmem,) * 6,
        scratch_shapes=[
            pltpu.VMEM((shard_rows, dim), BF16),
            pltpu.VMEM((2 * shard_rows + 8, dim), F32),
            pltpu.VMEM((2, half, dim), F32),
            pltpu.VMEM((2, chips, half, dim), BF16),
            pltpu.VMEM((2, dim, half), F32),
            pltpu.VMEM((2, 1, half), F32),
            pltpu.VMEM((dim, dim), F32),
            pltpu.VMEM((dim, hidden), BF16),
            pltpu.VMEM((dim, hidden), BF16),
            pltpu.VMEM((2, devs, dim, half), BF16),
            pltpu.VMEM((2, devs, dim, half), BF16),
            pltpu.VMEM((hidden, sub), BF16),
            pltpu.VMEM((hidden, sub), BF16),
            pltpu.VMEM((5, 2, dim, half), F32),
            pltpu.VMEM((chips, 2, 2, dim, half), F32),
            pltpu.VMEM((chips, 2, 2, dim, half), F32),
            dma((2,)),
            dma((2, chips - 1, 2)), dma((2, chips - 1, 2)),
            *gather_sems(1), *gather_sems(2), *gather_sems(4),
            dma((chips, 2)), dma((chips, 2)),
            dma((chips - 1, 2, 2)), dma((chips - 1, 2, 2)),
        ],
        compiler_params=pltpu.CompilerParams(
            collective_id=0, has_side_effects=True, vmem_limit_bytes=67043328,
        ),
        cost_estimate=pl.CostEstimate(flops=12 * tokens * hidden * dim, bytes_accessed=tokens * dim * 8,
                                      transcendentals=0),
        name="block",
    )(ids, ids.reshape(groups, dim), table, gain.reshape(1, dim), w_up.T, w_down, d_out)


def scatter_kernel(
    half_rows, extra,
    list_ref, count_ref, dx_ref, *refs,
):
    extra_in, grad_ref, extra_out = refs[:extra], refs[extra], refs[extra + 1:2 * extra + 1]
    acc, dx_in, dx_f32, in_sem, ex_sem = refs[2 * extra + 1:2 * extra + 6]
    extra_buf = refs[2 * extra + 6:]
    blocks, block = dx_in.shape[:2]
    groups, width = list_ref.shape
    tokens = dx_f32.shape[0]

    def load(b):
        return pltpu.make_async_copy(dx_ref.at[pl.ds(b * block, block)], dx_in.at[b], in_sem.at[b])

    def take(e):
        return pltpu.make_async_copy(extra_in[e], extra_buf[e], ex_sem.at[0, e])

    def give(e):
        return pltpu.make_async_copy(extra_buf[e], extra_out[e], ex_sem.at[1, e])

    for b in range(blocks):
        load(b).start()
    for e in range(extra):
        take(e).start()
    acc[...] = jnp.zeros(acc.shape, F32)
    conv = 128

    for b in range(blocks):
        load(b).wait()

        def convert(i, _):
            at = pl.multiple_of(i * conv, conv)
            dst = pl.multiple_of(b * block + i * conv, conv)
            dx_f32[pl.ds(dst, conv), :] = dx_in[b, pl.ds(at, conv), :].astype(F32)
            return 0

        lax.fori_loop(0, block // conv, convert, 0)
    for e in range(extra):
        take(e).wait()
        give(e).start()

    def group(g, _):
        start = g * width
        first = ((start // half_rows) % 2) * (tokens // 2) + (start // (2 * half_rows)) * half_rows + start % half_rows

        def one(i, _):
            packed = list_ref[g, i]
            tok = first + (packed & (width - 1))
            row = packed >> (width.bit_length() - 1)
            acc[pl.ds(row, 1), :] += dx_f32[pl.ds(tok, 1), :]
            return 0

        lax.fori_loop(0, count_ref[0, g], one, 0)
        return 0

    lax.fori_loop(0, groups, group, 0)
    copy = pltpu.make_async_copy(acc, grad_ref, in_sem.at[0])
    copy.start()
    for e in range(extra):
        give(e).wait()
    copy.wait()


def scatter_rows(half_rows, shard_rows, lists, counts, dx_all, others):
    tokens, dim = dx_all.shape
    smem = pl.BlockSpec(memory_space=pltpu.SMEM)
    hbm = pl.BlockSpec(memory_space=pltpu.HBM)
    blocks = 8
    extra = len(others)
    shapes = [jax.ShapeDtypeStruct((shard_rows, dim), F32)] + [jax.ShapeDtypeStruct(o.shape, o.dtype) for o in others]
    return pl.pallas_call(
        functools.partial(scatter_kernel, half_rows, extra),
        out_shape=tuple(shapes),
        in_specs=[smem, smem] + [hbm] * (1 + extra),
        out_specs=(hbm,) * (1 + extra),
        scratch_shapes=[
            pltpu.VMEM((shard_rows, dim), F32),
            pltpu.VMEM((blocks, tokens // blocks, dim), BF16),
            pltpu.VMEM((tokens, dim), F32),
            pltpu.SemaphoreType.DMA((blocks,)),
            pltpu.SemaphoreType.DMA((2, extra)),
            *[pltpu.VMEM(o.shape, o.dtype) for o in others],
        ],
        compiler_params=pltpu.CompilerParams(vmem_limit_bytes=67043328),
        name="scatter",
    )(lists, counts, dx_all, *others)


def solution(mesh):
    chips = mesh.shape["tp"] // 2

    def shard_body(token_ids, embed_table, norm_gain, w_up, w_down, d_out):
        shard_rows, dim = embed_table.shape
        block_out, dw1t, dw2, dx_all, lists, counts = run_block(
            chips, token_ids, embed_table, norm_gain, w_up, w_down, d_out)
        grad_table, block_out, dw1t, dw2 = scatter_rows(
            d_out.shape[0] // 2, shard_rows, lists, counts, dx_all.reshape(-1, dim), (block_out, dw1t, dw2))
        return block_out, grad_table, dw1t.T, dw2

    return jax.shard_map(
        shard_body,
        mesh=mesh,
        in_specs=(P("dp"), P("tp", None), P(), P(None, "tp"), P("tp", None), P(("dp", "tp"), None)),
        out_specs=(P(("dp", "tp"), None), P(("dp", "tp"), None), P("dp", "tp"), P(("dp", "tp"), None)),
        check_vma=False,
    )
```

time: 246 us -> 236 us (0.959)
  local copies, waits for them, and re-layouts: 12.8 us -> 0 us
  Pallas kernels: 230 us -> 235 us
  other arithmetic: 2.46 us -> 0 us
    unnamed x18 -> x0, local copies, waits for them, and re-layouts: 10.4 us -> none
    pallas_call x2, Pallas kernels: 230 us -> 235 us  [the longest x1 215 us: run_block(): pl.pallas_call(functools.partial(block_kernel, chips, sub, row_tiles(hidd...]
where the time goes in v2:
time: 236 us
  Pallas kernels  235 us (100%)
    pallas_call x1, Pallas kernels, run_block(): pl.pallas_call(functools.partial(block_kernel, chips, sub, row_tiles(hidd...  215 us
    pallas_call x1, Pallas kernels, scatter_rows(): pl.pallas_call(functools.partial(scatter_kernel, half_rows, extra), out_s...  20.1 us

profile of v2, /device:TPU:21, one launch (start us, length us, event | category | flops | bytes accessed | tf_op | source)
XLA Modules:
  0.0 236.1 jit_solution(17837193973909710180)
XLA Ops:
  0.6 215.4 %block.1 = (bf16[1024,128]{1,0:T(8,128)(2,1)}, f32[1184,128]{1,0:T(8,128)}, f32[1184,128]{1,0:T(8,128)}, bf16[2,16,512,128]{3,2,1,0:T(8,128)(2,1)}, s32[128,128]{1,0:T(8,128)}, /*index=5*/s32[8,128]{1,0:T(8,128)}) custom-call(s32[16384]{0:T(1024)} %ids_ref.1, s32[128,128]{1,0:T(8,128)} %bitcast.8, bf16[9504,128]{1,0:T(8,128)(2,1)} %table_ref.1, ...), custom_call_target="tpu_custom_call" | custom-call | flops 29796335616 | bytes 16777216 | tf_op jit(solution)/shard_map/block/pallas_call | solution.py:408
  216.0 20.1 %scatter.1 = (f32[9504,128]{1,0:T(8,128)}, bf16[1024,128]{1,0:T(8,128)(2,1)}, f32[1184,128]{1,0:T(8,128)}, f32[1184,128]{1,0:T(8,128)}) custom-call(s32[128,128]{1,0:T(8,128)} %get-tuple-element.14.list_ref, s32[8,128]{1,0:T(8,128)} %get-tuple-element.15.count_ref, bf16[16384,128]{1,0:T(8,128)(2,1)} %bitcast.5, bf16[1024,128]{1,0:T(8,128)(2,1)} %get-tuple-element.17.refs_0_, ...), custom_call_target="tpu_custom_call" | custom-call | tf_op jit(solution)/shard_map/scatter/pallas_call | solution.py:522

commit v3 on v2

--- a/solution.py
+++ b/solution.py
@@ -10,6 +10,7 @@
 NORM_EPS = 1e-6
 GELU_C = 0.7978845608028654
 GELU_A = 0.044715
+BUNCH = 4
 MESH = pl.DeviceIdType.MESH
 F32 = jnp.float32
 BF16 = jnp.bfloat16
@@ -23,11 +24,13 @@
 
 
 def block_kernel(
-    chips, sub, tiles,
-    ids_ref, ids_vec, table_ref, gain_ref, w1t_ref, w2_ref, dout_ref,
+    chips, tiles,
+    ids_ref, ids_vec, table_hbm, gain_ref, w1t_ref, w2_ref, dout_ref,
+    out_hbm, dw1t_hbm, dw2_hbm, dx_hbm, list_hbm, count_hbm,
     out_ref, dw1t_ref, dw2_ref, dx_all, list_ref, count_ref,
-    tab_in, tab_f32, gath, xs, x_t, inv_r, gain_t, w1_ref, w2t_ref, d_all, n_all, h_buf, du_buf, parts, precv, rs,
-    tab_sem, x_send, x_recv, d_send, d_recv, dp_send, dp_recv, n_send, n_recv, np_send, np_recv,
+    table_ref, tab_in, tab_f32, gath, xs, x_t, inv_r, gain_t, w1_ref, w2t_ref, d_all, n_all,
+    h_a, h_b, du_a, du_b, parts, precv, rs,
+    tab_sem, put_sem, dx_sem, x_send, x_recv, d_send, d_recv, dp_send, dp_recv, n_send, n_recv, np_send, np_recv,
     e_send, e_recv, ep_send, ep_recv, p_send, p_recv, r_send, r_recv,
 ):
     me = lax.axis_index("tp")
@@ -45,6 +48,8 @@
     def chip_at(half, hop):
         return (chip + (1 - half) * (chips - hop) + half * hop) % chips
 
+    tab_load = pltpu.make_async_copy(table_hbm, table_ref, tab_sem.at[2])
+    tab_load.start()
     barrier = pltpu.get_barrier_semaphore()
     for dev in (partner, up, down):
         pl.semaphore_signal(barrier, inc=1, device_id={"tp": dev}, device_id_type=MESH)
@@ -106,7 +111,7 @@
     n_sems = (n_send, n_recv, np_send, np_recv)
     e_sems = (e_send, e_recv, ep_send, ep_recv)
 
-    tab_copy = remote(table_ref, tab_in, tab_sem.at[0], tab_sem.at[1], partner)
+    tab_copy = remote(table_hbm, tab_in, tab_sem.at[0], tab_sem.at[1], partner)
     tab_copy.start()
     for half in (0, 1):
         rows = dout_ref[half * half_rows:(half + 1) * half_rows, :].astype(F32)
@@ -123,10 +128,13 @@
 
         lax.fori_loop(0, shard_rows // conv, body, 0)
 
+    tab_load.wait()
     convert(table_ref, core * shard_rows)
     tab_f32[pl.ds(2 * shard_rows, 8), :] = jnp.zeros((8, dim), F32)
+    gather_step(d_all, d_sems, 0)
     tab_copy.wait()
     convert(tab_in, (1 - core) * shard_rows)
+    gather_step(d_all, d_sems, 1)
 
     pieces = x_send.shape[2]
     size = half_rows // pieces
@@ -170,9 +178,9 @@
                 def _():
                     x_copy(half, step, piece).start()
 
-        @pl.when(step < steps)
+        @pl.when(step + 2 < steps)
         def _():
-            gather_step(d_all, d_sems, step)
+            gather_step(d_all, d_sems, step + 2)
 
         @pl.when(step == 0)
         def _():
@@ -194,10 +202,12 @@
         owned = ((rel >= 0) & (rel < shard_rows)).astype(F32).astype(BF16)
         nt = (((1,), (1,)), ((), ()))
         ones = jnp.ones((8, ids_vec.shape[1]), BF16)
-        count_ref[...] = lax.dot_general(ones, owned, nt, preferred_element_type=F32).astype(jnp.int32)
+        counts = lax.dot_general(ones, owned, nt, preferred_element_type=F32).astype(jnp.int32)
+        count_ref[...] = (counts + (BUNCH - 1)) // BUNCH
 
     groups = ids_vec.shape[0]
     width = ids_vec.shape[1]
+    tokens = groups * width
     batch = 8
     turns = groups // batch
     per_step = -(-turns // steps)
@@ -217,6 +227,7 @@
             rank = jnp.dot(owned.astype(F32).astype(BF16), before, preferred_element_type=F32).astype(jnp.int32)
             rank = jnp.where(owned, rank, -1)
             rel = jnp.where(owned, rel, 0)
+            count = jnp.sum(owned.astype(F32), axis=1, keepdims=True).astype(jnp.int32)
             lines = []
             for g in range(batch):
                 hot = (jnp.broadcast_to(rank[g:g + 1], (width, width)) == place).astype(F32).astype(BF16)
@@ -224,7 +235,11 @@
                 vals = jnp.where(sub8 == 0, lane[:8], jnp.where(sub8 == 1, row // width, row % width))
                 got = lax.dot_general(vals.astype(F32).astype(BF16), hot, nt, preferred_element_type=F32)
                 got = got.astype(jnp.int32)
-                lines.append((got[1:2] * width + got[2:3]) * width + got[0:1])
+                start = (t * batch + g) * width
+                place_0 = (((start // half_rows) % 2) * (tokens // 2) + (start // (2 * half_rows)) * half_rows
+                           + start % half_rows)
+                line = (got[1:2] * width + got[2:3]) * tokens + (got[0:1] + place_0)
+                lines.append(jnp.where(lane[:1] < count[g:g + 1], line, shard_rows * tokens))
             list_ref[pl.ds(at, batch), :] = jnp.concatenate(lines, axis=0)
             return 0
 
@@ -253,50 +268,66 @@
     nt = (((1,), (1,)), ((), ()))
 
     def mlp(half, blk, dst):
-        def body(i, _):
-            cols = pl.ds(pl.multiple_of(i * sub, sub), sub)
-            n_t = n_all[half, blk, :, cols]
-            d_t = d_all[half, blk, :, cols]
-            for lo, hi in tiles:
-                u = jnp.dot(w1t_ref[lo:hi], n_t, preferred_element_type=F32).astype(BF16).astype(F32)
-                dh = jnp.dot(w2_ref[lo:hi], d_t, preferred_element_type=F32)
-                sq = (GELU_C * GELU_A) * (u * u)
-                th = jnp.tanh(u * (GELU_C + sq))
-                sg = 0.5 + 0.5 * th
-                h = u * sg
-                slope = sg + (h * (1.0 - th)) * (GELU_C + 3.0 * sq)
-                h_buf[lo:hi] = h.astype(BF16)
-                du_buf[lo:hi] = (dh * slope).astype(BF16)
-            h = h_buf[...]
-            du = du_buf[...]
-            dst[0, :, cols] = jnp.dot(w2t_ref[...], h, preferred_element_type=F32)
-            dst[1, :, cols] = jnp.dot(w1_ref[...], du, preferred_element_type=F32)
-            dw2_ref[...] += lax.dot_general(h, d_t, nt, preferred_element_type=F32)
-            dw1t_ref[...] += lax.dot_general(du, n_t, nt, preferred_element_type=F32)
-            return 0
-
-        lax.fori_loop(0, half_rows // sub, body, 0)
+        sub = half_rows // 2
+        left, right = slice(0, sub), slice(sub, 2 * sub)
+
+        def front(lo, hi, cols, h_buf, du_buf):
+            u = jnp.dot(w1t_ref[lo:hi], n_all[half, blk, :, cols], preferred_element_type=F32).astype(BF16).astype(F32)
+            dh = jnp.dot(w2_ref[lo:hi], d_all[half, blk, :, cols], preferred_element_type=F32)
+            sq = (GELU_C * GELU_A) * (u * u)
+            th = jnp.tanh(u * (GELU_C + sq))
+            sg = 0.5 + 0.5 * th
+            h = u * sg
+            slope = sg + (h * (1.0 - th)) * (GELU_C + 3.0 * sq)
+            h_buf[lo:hi] = h.astype(BF16)
+            du_buf[lo:hi] = (dh * slope).astype(BF16)
+
+        def weights(lo, hi, cols, h_buf, du_buf):
+            n_t, d_t = n_all[half, blk, :, cols], d_all[half, blk, :, cols]
+            dw2_ref[lo:hi] += lax.dot_general(h_buf[lo:hi], d_t, nt, preferred_element_type=F32)
+            dw1t_ref[lo:hi] += lax.dot_general(du_buf[lo:hi], n_t, nt, preferred_element_type=F32)
+
+        def back(cols, h_buf, du_buf):
+            dst[0, :, cols] = jnp.dot(w2t_ref[...], h_buf[...], preferred_element_type=F32)
+            dst[1, :, cols] = jnp.dot(w1_ref[...], du_buf[...], preferred_element_type=F32)
+
+        for lo, hi in tiles:
+            front(lo, hi, left, h_a, du_a)
+        for lo, hi in tiles:
+            weights(lo, hi, left, h_a, du_a)
+            front(lo, hi, right, h_b, du_b)
+        back(left, h_a, du_a)
+        for lo, hi in tiles:
+            weights(lo, hi, right, h_b, du_b)
+        back(right, h_b, du_b)
+
+    def order_of(half, hop):
+        return (hop + half * (chips - 1)) % chips
 
     def p_copy(half, hop):
-        return remote(parts.at[(hop % 2) * 2 + half], precv.at[hop, half], p_send.at[hop, half], p_recv.at[hop, half],
-                      partner)
+        return remote(parts.at[(order_of(half, hop) % 2) * 2 + half], precv.at[hop, half], p_send.at[hop, half],
+                      p_recv.at[hop, half], partner)
 
     def r_copy(half, val, step):
         return remote(rs.at[step, half, val], rs.at[step + 1, half, val], r_send.at[step, half, val],
                       r_recv.at[step, half, val], next_dev(half))
 
     def part(g, _):
-        early = jnp.where(g < 2, 1, 0)
-        turn = jnp.maximum(g - 2, 0)
-        step = jnp.where(g < 2, steps, turn // 4)
-        late = jnp.where((g >= 2) & (step == steps), 1, 0)
-        mine = jnp.where(g < 2, 0, jnp.maximum((turn % 4) // 2, late))
-        half = g % 2
+        turn = jnp.maximum(g - 1, 0)
+        own_chip = jnp.where((g == 0) | (turn >= 4 * steps), 1, 0)
+        late = turn - 4 * steps
+        step = jnp.where(own_chip == 1, steps, turn // 4)
+        half = jnp.where(own_chip == 1, jnp.where((late == 0) | (late == 2), 1, 0), (turn % 4) // 2)
+        mine = jnp.where(own_chip == 1, jnp.where(late >= 1, 1, 0), turn % 2)
         hop = (step + 1) % chips
         blk = chip_at(half, hop) * 2 + (1 - core) * (1 - mine) + core * mine
 
-        ahead = turn // 2
-        @pl.when((early == 0) & (half == 0) & (ahead < steps))
+        lead = min(3, steps)
+        early = (g == 1) | ((g == 2) & (lead > 1)) | ((g == 4) & (lead > 2))
+        steady = (turn % 4 == 0) & (turn >= 8) & (turn // 4 + 1 < steps)
+        ahead = jnp.where(early, jnp.where(g == 4, 2, g - 1), turn // 4 + 1)
+
+        @pl.when(early | steady)
         def _():
             gather_step(n_all, n_sems, ahead)
 
@@ -304,11 +335,11 @@
         def _():
             pair_arrival(n_all, np_send, np_recv, half, hop).wait_recv()
 
-            @pl.when(hop >= 2)
+            @pl.when(order_of(half, hop) >= 2)
             def _():
-                p_copy(half, hop - 2).wait_send()
-
-        spot = jnp.where(mine == 0, (hop % 2) * 2 + half, 4)
+                p_copy(half, (hop + chips - 2) % chips).wait_send()
+
+        spot = jnp.where(mine == 0, (order_of(half, hop) % 2) * 2 + half, 4)
         mlp(half, blk, parts.at[spot])
 
         @pl.when(mine == 0)
@@ -335,6 +366,18 @@
         return 0
 
     lax.fori_loop(0, 4 * chips, part, 0)
+
+    puts = [
+        pltpu.make_async_copy(src, dst, put_sem.at[i])
+        for i, (src, dst) in enumerate((
+            (dw1t_ref, dw1t_hbm), (dw2_ref, dw2_hbm), (list_ref, list_hbm), (count_ref, count_hbm), (out_ref, out_hbm),
+        ))
+    ]
+    for put in puts[:4]:
+        put.start()
+
+    def dx_put(half, blk):
+        return pltpu.make_async_copy(dx_all.at[half, blk], dx_hbm.at[half, blk], dx_sem.at[half, blk])
 
     gain = jnp.concatenate([gain_t[...]] * (half_rows // dim), axis=1)
     for half in (0, 1):
@@ -347,12 +390,23 @@
         dx = dout_ref[rows, :].astype(F32) + dx.T
         dx_all[half, me] = dx.astype(BF16)
         gather_begin(dx_all, e_sems, half)
+        dx_put(half, me).start()
     for half in (0, 1):
         rows = slice(half * half_rows, (half + 1) * half_rows)
         out_ref[rows, :] = (x_t[half] + rs[steps, half, 0]).T.astype(BF16)
 
+    puts[4].start()
+
+    def pair_done(hop):
+        for half in (0, 1):
+            pair_arrival(dx_all, ep_send, ep_recv, half, hop).wait_recv()
+            dx_put(half, chip_at(half, hop) * 2 + 1 - core).start()
+
     def e_step(step, _):
         gather_step(dx_all, e_sems, step)
+        for half in (0, 1):
+            dx_put(half, chip_at(half, step + 1) * 2 + core).start()
+        pair_done(step)
         return 0
 
     lax.fori_loop(0, steps, e_step, 0)
@@ -370,23 +424,26 @@
 
     lax.fori_loop(0, steps, drain, 0)
     for half in (0, 1):
-        for hop in (chips - 2, chips - 1):
-            p_copy(half, hop).wait_send()
+        for order in (chips - 2, chips - 1):
+            p_copy(half, (order + half) % chips).wait_send()
+    for put in puts:
+        put.wait()
+    pair_done(steps)
     gather_drain(dx_all, e_sems)
 
-    def e_wait(hop, _):
+    def put_wait(blk, _):
         for half in (0, 1):
-            pair_arrival(dx_all, ep_send, ep_recv, half, hop).wait_recv()
+            dx_put(half, blk).wait()
         return 0
 
-    lax.fori_loop(0, chips, e_wait, 0)
+    lax.fori_loop(0, 2 * chips, put_wait, 0)
 
 
 def row_tiles(hidden):
-    if hidden < 256:
-        return ((0, hidden),)
-    cut = (hidden // 2) // 16 * 16
-    return ((0, cut), (cut, hidden))
+    count = 4 if hidden >= 512 else 1
+    cut = -(-hidden // (16 * count)) * 16
+    edges = [min(i * cut, hidden) for i in range(count)] + [hidden]
+    return tuple(zip(edges[:-1], edges[1:]))
 
 
 def run_block(chips, ids, table, gain, w_up, w_down, d_out):
@@ -395,7 +452,7 @@
     hidden = w_down.shape[0]
     half = rows // 2
     devs = 2 * chips
-    sub = min(256, half)
+    sub = half // 2
     dma = pltpu.SemaphoreType.DMA
     vmem = pl.BlockSpec(memory_space=pltpu.VMEM)
     tokens = rows * devs
@@ -405,19 +462,23 @@
         ring, pair = (2, chips - 1, pieces), (2, chips)
         return [dma(ring), dma(ring), dma(pair), dma(pair)]
 
+    results = (
+        jax.ShapeDtypeStruct((rows, dim), BF16),
+        jax.ShapeDtypeStruct((hidden, dim), F32),
+        jax.ShapeDtypeStruct((hidden, dim), F32),
+        jax.ShapeDtypeStruct((2, devs, half, dim), BF16),
+        jax.ShapeDtypeStruct((groups, dim), jnp.int32),
+        jax.ShapeDtypeStruct((8, groups), jnp.int32),
+    )
+    hbm = pl.BlockSpec(memory_space=pltpu.HBM)
     return pl.pallas_call(
-        functools.partial(block_kernel, chips, sub, row_tiles(hidden)),
-        out_shape=(
-            jax.ShapeDtypeStruct((rows, dim), BF16),
-            jax.ShapeDtypeStruct((hidden, dim), F32),
-            jax.ShapeDtypeStruct((hidden, dim), F32),
-            jax.ShapeDtypeStruct((2, devs, half, dim), BF16),
-            jax.ShapeDtypeStruct((groups, dim), jnp.int32),
-            jax.ShapeDtypeStruct((8, groups), jnp.int32),
-        ),
-        in_specs=[pl.BlockSpec(memory_space=pltpu.SMEM)] + [vmem] * 6,
-        out_specs=(vmem,) * 6,
+        functools.partial(block_kernel, chips, row_tiles(hidden)),
+        out_shape=results,
+        in_specs=[pl.BlockSpec(memory_space=pltpu.SMEM), vmem, hbm] + [vmem] * 4,
+        out_specs=(hbm,) * 6,
         scratch_shapes=[
+            *[pltpu.VMEM(r.shape, r.dtype) for r in results],
+            pltpu.VMEM((shard_rows, dim), BF16),
             pltpu.VMEM((shard_rows, dim), BF16),
             pltpu.VMEM((2 * shard_rows + 8, dim), F32),
             pltpu.VMEM((2, half, dim), F32),
@@ -429,12 +490,11 @@
             pltpu.VMEM((dim, hidden), BF16),
             pltpu.VMEM((2, devs, dim, half), BF16),
             pltpu.VMEM((2, devs, dim, half), BF16),
-            pltpu.VMEM((hidden, sub), BF16),
-            pltpu.VMEM((hidden, sub), BF16),
+            *[pltpu.VMEM((hidden, sub), BF16)] * 4,
             pltpu.VMEM((5, 2, dim, half), F32),
             pltpu.VMEM((chips, 2, 2, dim, half), F32),
             pltpu.VMEM((chips, 2, 2, dim, half), F32),
-            dma((2,)),
+            dma((3,)), dma((5,)), dma((2, devs)),
             dma((2, chips - 1, 2)), dma((2, chips - 1, 2)),
             *gather_sems(1), *gather_sems(2), *gather_sems(4),
             dma((chips, 2)), dma((chips, 2)),
@@ -449,16 +509,15 @@
     )(ids, ids.reshape(groups, dim), table, gain.reshape(1, dim), w_up.T, w_down, d_out)
 
 
-def scatter_kernel(
-    half_rows, extra,
-    list_ref, count_ref, dx_ref, *refs,
-):
+def scatter_kernel(extra, list_hbm, count_hbm, dx_ref, *refs):
     extra_in, grad_ref, extra_out = refs[:extra], refs[extra], refs[extra + 1:2 * extra + 1]
-    acc, dx_in, dx_f32, in_sem, ex_sem = refs[2 * extra + 1:2 * extra + 6]
-    extra_buf = refs[2 * extra + 6:]
+    acc, dx_in, dx_f32, list_ref, count_ref, in_sem, ex_sem, small_sem = refs[2 * extra + 1:2 * extra + 9]
+    extra_buf = refs[2 * extra + 9:]
     blocks, block = dx_in.shape[:2]
-    groups, width = list_ref.shape
+    groups = list_ref.shape[0]
     tokens = dx_f32.shape[0]
+    shard_rows = grad_ref.shape[0]
+    shift = tokens.bit_length() - 1
 
     def load(b):
         return pltpu.make_async_copy(dx_ref.at[pl.ds(b * block, block)], dx_in.at[b], in_sem.at[b])
@@ -469,6 +528,12 @@
     def give(e):
         return pltpu.make_async_copy(extra_buf[e], extra_out[e], ex_sem.at[1, e])
 
+    small = (
+        pltpu.make_async_copy(list_hbm, list_ref, small_sem.at[0]),
+        pltpu.make_async_copy(count_hbm, count_ref, small_sem.at[1]),
+    )
+    for copy in small:
+        copy.start()
     for b in range(blocks):
         load(b).start()
     for e in range(extra):
@@ -489,47 +554,47 @@
     for e in range(extra):
         take(e).wait()
         give(e).start()
+    for copy in small:
+        copy.wait()
 
     def group(g, _):
-        start = g * width
-        first = ((start // half_rows) % 2) * (tokens // 2) + (start // (2 * half_rows)) * half_rows + start % half_rows
-
-        def one(i, _):
-            packed = list_ref[g, i]
-            tok = first + (packed & (width - 1))
-            row = packed >> (width.bit_length() - 1)
-            acc[pl.ds(row, 1), :] += dx_f32[pl.ds(tok, 1), :]
+        def bunch(i, _):
+            for j in range(BUNCH):
+                packed = list_ref[g, i * BUNCH + j]
+                acc[pl.ds(packed >> shift, 1), :] += dx_f32[pl.ds(packed & (tokens - 1), 1), :]
             return 0
 
-        lax.fori_loop(0, count_ref[0, g], one, 0)
+        lax.fori_loop(0, count_ref[0, g], bunch, 0)
         return 0
 
     lax.fori_loop(0, groups, group, 0)
-    copy = pltpu.make_async_copy(acc, grad_ref, in_sem.at[0])
+    copy = pltpu.make_async_copy(acc.at[pl.ds(0, shard_rows)], grad_ref, in_sem.at[0])
     copy.start()
     for e in range(extra):
         give(e).wait()
     copy.wait()
 
 
-def scatter_rows(half_rows, shard_rows, lists, counts, dx_all, others):
+def scatter_rows(shard_rows, lists, counts, dx_all, others):
     tokens, dim = dx_all.shape
-    smem = pl.BlockSpec(memory_space=pltpu.SMEM)
     hbm = pl.BlockSpec(memory_space=pltpu.HBM)
     blocks = 8
     extra = len(others)
     shapes = [jax.ShapeDtypeStruct((shard_rows, dim), F32)] + [jax.ShapeDtypeStruct(o.shape, o.dtype) for o in others]
     return pl.pallas_call(
-        functools.partial(scatter_kernel, half_rows, extra),
+        functools.partial(scatter_kernel, extra),
         out_shape=tuple(shapes),
-        in_specs=[smem, smem] + [hbm] * (1 + extra),
+        in_specs=[hbm] * (3 + extra),
         out_specs=(hbm,) * (1 + extra),
         scratch_shapes=[
-            pltpu.VMEM((shard_rows, dim), F32),
+            pltpu.VMEM((shard_rows + 8, dim), F32),
             pltpu.VMEM((blocks, tokens // blocks, dim), BF16),
             pltpu.VMEM((tokens, dim), F32),
+            pltpu.SMEM(lists.shape, jnp.int32),
+            pltpu.SMEM(counts.shape, jnp.int32),
             pltpu.SemaphoreType.DMA((blocks,)),
             pltpu.SemaphoreType.DMA((2, extra)),
+            pltpu.SemaphoreType.DMA((2,)),
             *[pltpu.VMEM(o.shape, o.dtype) for o in others],
         ],
         compiler_params=pltpu.CompilerParams(vmem_limit_bytes=67043328),
@@ -545,7 +610,7 @@
         block_out, dw1t, dw2, dx_all, lists, counts = run_block(
             chips, token_ids, embed_table, norm_gain, w_up, w_down, d_out)
         grad_table, block_out, dw1t, dw2 = scatter_rows(
-            d_out.shape[0] // 2, shard_rows, lists, counts, dx_all.reshape(-1, dim), (block_out, dw1t, dw2))
+            shard_rows, lists, counts, dx_all.reshape(-1, dim), (block_out, dw1t, dw2))
         return block_out, grad_table, dw1t.T, dw2
 
     return jax.shard_map(

time: 236 us -> 217 us (0.919)
  Pallas kernels: 235 us -> 217 us
    pallas_call x2, Pallas kernels: 235 us -> 217 us  [the longest x1 204 us: run_block(): pl.pallas_call(functools.partial(block_kernel, chips, row_tiles(hidden)),...]
where the time goes in v3:
time: 217 us
  Pallas kernels  217 us (100%)
    pallas_call x1, Pallas kernels, run_block(): pl.pallas_call(functools.partial(block_kernel, chips, row_tiles(hidden)),...  204 us
    pallas_call x1, Pallas kernels, scatter_rows(): pl.pallas_call(functools.partial(scatter_kernel, extra), out_shape=tuple(...  12.7 us

profile of v3, /device:TPU:21, one launch (start us, length us, event | category | flops | bytes accessed | tf_op | source)
XLA Modules:
  0.0 217.2 jit_solution(7628656745223203488)
XLA Ops:
  0.6 203.8 %block.1 = (bf16[1024,128]{1,0:T(8,128)(2,1)}, f32[1184,128]{1,0:T(8,128)}, f32[1184,128]{1,0:T(8,128)}, bf16[2,16,512,128]{3,2,1,0:T(8,128)(2,1)}, s32[128,128]{1,0:T(8,128)}, /*index=5*/s32[8,128]{1,0:T(8,128)}) custom-call(s32[16384]{0:T(1024)} %ids_ref.1, s32[128,128]{1,0:T(8,128)} %bitcast.8, bf16[9504,128]{1,0:T(8,128)(2,1)} %table_hbm.1, ...), custom_call_target="tpu_custom_call" | custom-call | flops 29796335616 | bytes 16777216 | tf_op jit(solution)/shard_map/block/pallas_call | solution.py:474
  204.5 12.7 %scatter.1 = (f32[9504,128]{1,0:T(8,128)}, bf16[1024,128]{1,0:T(8,128)(2,1)}, f32[1184,128]{1,0:T(8,128)}, f32[1184,128]{1,0:T(8,128)}) custom-call(s32[128,128]{1,0:T(8,128)} %get-tuple-element.14.list_hbm, s32[8,128]{1,0:T(8,128)} %get-tuple-element.15.count_hbm, bf16[16384,128]{1,0:T(8,128)(2,1)} %bitcast.5, bf16[1024,128]{1,0:T(8,128)(2,1)} %get-tuple-element.17.refs_0_, ...), custom_call_target="tpu_custom_call" | custom-call | tf_op jit(solution)/shard_map/scatter/pallas_call | solution.py:584

commit v4 on v3

--- a/solution.py
+++ b/solution.py
@@ -30,8 +30,8 @@
     out_ref, dw1t_ref, dw2_ref, dx_all, list_ref, count_ref,
     table_ref, tab_in, tab_f32, gath, xs, x_t, inv_r, gain_t, w1_ref, w2t_ref, d_all, n_all,
     h_a, h_b, du_a, du_b, parts, precv, rs,
-    tab_sem, put_sem, dx_sem, x_send, x_recv, d_send, d_recv, dp_send, dp_recv, n_send, n_recv, np_send, np_recv,
-    e_send, e_recv, ep_send, ep_recv, p_send, p_recv, r_send, r_recv,
+    tab_sem, put_sem, dx_sem, x_send, x_recv, d_send, d_recv, dp_recv, n_send, n_recv, np_recv,
+    e_send, e_recv, ep_recv, p_send, p_recv, r_send, r_recv,
 ):
     me = lax.axis_index("tp")
     chip, core = me // 2, me % 2
@@ -57,28 +57,27 @@
 
     def ring_copy(buf, send, recv, half, hop, step, piece):
         blk = chip_at(half, hop) * 2 + core
-        pieces = send.shape[2]
-        size = buf.shape[2] // pieces
+        size = buf.shape[2] // recv.shape[2]
         ref = buf.at[half, blk, pl.ds(piece * size, size)]
-        return remote(ref, ref, send.at[half, step, piece], recv.at[half, step, piece], next_dev(half))
+        return remote(ref, ref, send.at[0], recv.at[half, step, piece], next_dev(half))
 
     def pair_copy(buf, send, recv, half, hop):
         blk = chip_at(half, hop) * 2 + core
-        return remote(buf.at[half, blk], buf.at[half, blk], send.at[half, hop], recv.at[half, hop], partner)
+        return remote(buf.at[half, blk], buf.at[half, blk], send.at[1], recv.at[half, hop], partner)
 
     def pair_arrival(buf, send, recv, half, hop):
         blk = chip_at(half, hop) * 2 + 1 - core
-        return remote(buf.at[half, blk], buf.at[half, blk], send.at[half, hop], recv.at[half, hop], partner)
+        return remote(buf.at[half, blk], buf.at[half, blk], send.at[1], recv.at[half, hop], partner)
 
     def gather_begin(buf, sems, half):
-        send, recv, psend_, precv_ = sems
-        for piece in range(send.shape[2]):
+        send, recv, pair_recv = sems
+        for piece in range(recv.shape[2]):
             ring_copy(buf, send, recv, half, 0, 0, piece).start()
-        pair_copy(buf, psend_, precv_, half, 0).start()
+        pair_copy(buf, send, pair_recv, half, 0).start()
 
     def gather_step(buf, sems, step):
-        send, recv, psend_, precv_ = sems
-        for piece in range(send.shape[2]):
+        send, recv, pair_recv = sems
+        for piece in range(recv.shape[2]):
             for half in (0, 1):
                 ring_copy(buf, send, recv, half, step + 1, step, piece).wait_recv()
 
@@ -87,29 +86,18 @@
                     ring_copy(buf, send, recv, half, step + 1, step + 1, piece).start()
 
         for half in (0, 1):
-            pair_copy(buf, psend_, precv_, half, step + 1).start()
+            pair_copy(buf, send, pair_recv, half, step + 1).start()
 
     def gather_drain(buf, sems):
-        send, recv, psend_, precv_ = sems
-
-        def body(step, _):
-            for half in (0, 1):
-                for piece in range(send.shape[2]):
-                    ring_copy(buf, send, recv, half, step, step, piece).wait_send()
-            return 0
-
-        lax.fori_loop(0, steps, body, 0)
-
-        def pair_body(hop, _):
-            for half in (0, 1):
-                pair_copy(buf, psend_, precv_, half, hop).wait_send()
-            return 0
-
-        lax.fori_loop(0, chips, pair_body, 0)
-
-    d_sems = (d_send, d_recv, dp_send, dp_recv)
-    n_sems = (n_send, n_recv, np_send, np_recv)
-    e_sems = (e_send, e_recv, ep_send, ep_recv)
+        send, recv, pair_recv = sems
+        ring = buf.at[:, pl.ds(0, steps)]
+        pair = buf.at[:, pl.ds(0, chips)]
+        remote(ring, ring, send.at[0], recv.at[0, 0, 0], partner).wait_send()
+        remote(pair, pair, send.at[1], pair_recv.at[0, 0], partner).wait_send()
+
+    d_sems = (d_send, d_recv, dp_recv)
+    n_sems = (n_send, n_recv, np_recv)
+    e_sems = (e_send, e_recv, ep_recv)
 
     tab_copy = remote(table_hbm, tab_in, tab_sem.at[0], tab_sem.at[1], partner)
     tab_copy.start()
@@ -131,17 +119,18 @@
     tab_load.wait()
     convert(table_ref, core * shard_rows)
     tab_f32[pl.ds(2 * shard_rows, 8), :] = jnp.zeros((8, dim), F32)
-    gather_step(d_all, d_sems, 0)
     tab_copy.wait()
     convert(tab_in, (1 - core) * shard_rows)
-    gather_step(d_all, d_sems, 1)
-
-    pieces = x_send.shape[2]
+    tail = max(steps - 3, 0)
+    if tail > 0:
+        gather_step(d_all, d_sems, 0)
+
+    pieces = x_recv.shape[2]
     size = half_rows // pieces
 
     def x_copy(half, step, piece):
         rows = pl.ds(piece * size, size)
-        return remote(xs.at[half, step, rows], xs.at[half, step + 1, rows], x_send.at[half, step, piece],
+        return remote(xs.at[half, step, rows], xs.at[half, step + 1, rows], x_send.at[0],
                       x_recv.at[half, step, piece], next_dev(half))
 
     unroll = 8
@@ -178,17 +167,13 @@
                 def _():
                     x_copy(half, step, piece).start()
 
-        @pl.when(step + 2 < steps)
-        def _():
-            gather_step(d_all, d_sems, step + 2)
+        @pl.when(step + 1 < tail)
+        def _():
+            gather_step(d_all, d_sems, step + 1)
 
         @pl.when(step == 0)
         def _():
             setup()
-
-        @pl.when(step > 0)
-        def _():
-            owned_lists(step)
 
         return 0
 
@@ -258,13 +243,6 @@
         n_all[half, me] = (rows_t * inv * gain).astype(BF16)
         gather_begin(n_all, n_sems, half)
 
-    def d_wait(hop, _):
-        for half in (0, 1):
-            pair_arrival(d_all, dp_send, dp_recv, half, hop).wait_recv()
-        return 0
-
-    lax.fori_loop(0, chips, d_wait, 0)
-
     nt = (((1,), (1,)), ((), ()))
 
     def mlp(half, blk, dst):
@@ -309,7 +287,7 @@
                       p_recv.at[hop, half], partner)
 
     def r_copy(half, val, step):
-        return remote(rs.at[step, half, val], rs.at[step + 1, half, val], r_send.at[step, half, val],
+        return remote(rs.at[step, half, val], rs.at[step + 1, half, val], r_send.at[0],
                       r_recv.at[step, half, val], next_dev(half))
 
     def part(g, _):
@@ -331,15 +309,20 @@
         def _():
             gather_step(n_all, n_sems, ahead)
 
+        @pl.when((g <= 1) | (g == 5))
+        def _():
+            gather_step(d_all, d_sems, tail + jnp.where(g == 5, 2, g))
+
         @pl.when(mine == 0)
         def _():
-            pair_arrival(n_all, np_send, np_recv, half, hop).wait_recv()
+            pair_arrival(n_all, n_send, np_recv, half, hop).wait_recv()
+            pair_arrival(d_all, d_send, dp_recv, half, hop).wait_recv()
 
             @pl.when(order_of(half, hop) >= 2)
             def _():
                 p_copy(half, (hop + chips - 2) % chips).wait_send()
 
-        spot = jnp.where(mine == 0, (order_of(half, hop) % 2) * 2 + half, 4)
+        spot = jnp.where(mine == 0, (order_of(half, hop) % 2) * 2 + half, 4 + half)
         mlp(half, blk, parts.at[spot])
 
         @pl.when(mine == 0)
@@ -349,21 +332,46 @@
         @pl.when(mine == 1)
         def _():
             p_copy(half, hop).wait_recv()
-            for val in (0, 1):
+            for val in (1, 0):
                 @pl.when(step == 0)
                 def _():
-                    rs[step, half, val] = parts[4, val] + precv[hop, half, val]
-
-                @pl.when(step > 0)
+                    rs[step, half, val] = parts[4 + half, val] + precv[hop, half, val]
+
+                @pl.when((step > 0) & ((step < steps) | (val == 1)))
                 def _():
                     r_copy(half, val, step - 1).wait_recv()
-                    rs[step, half, val] = rs[step, half, val] + (parts[4, val] + precv[hop, half, val])
+                    rs[step, half, val] = rs[step, half, val] + (parts[4 + half, val] + precv[hop, half, val])
 
                 @pl.when(step < steps)
                 def _():
                     r_copy(half, val, step).start()
 
+                if val == 1:
+                    @pl.when(step == steps)
+                    def _():
+                        finish_dx(half)
+
+            @pl.when((step < steps) & (half == 1))
+            def _():
+                owned_lists(step + 1)
+
         return 0
+
+    def dx_put(half, blk):
+        return pltpu.make_async_copy(dx_all.at[half, blk], dx_hbm.at[half, blk], dx_sem.at[0])
+
+    def finish_dx(half):
+        gain = jnp.concatenate([gain_t[...]] * (half_rows // dim), axis=1)
+        xv = x_t[half]
+        inv = inv_r[half]
+        rows = pl.ds(pl.multiple_of(half * half_rows, half_rows), half_rows)
+        scaled = rs[steps, half, 1] * gain
+        mean = jnp.mean(xv * scaled, axis=0, keepdims=True)
+        dx = inv * (scaled - xv * inv * inv * mean)
+        dx = dout_ref[rows, :].astype(F32) + dx.T
+        dx_all[half, me] = dx.astype(BF16)
+        gather_begin(dx_all, e_sems, half)
+        dx_put(half, me).start()
 
     lax.fori_loop(0, 4 * chips, part, 0)
 
@@ -376,30 +384,17 @@
     for put in puts[:4]:
         put.start()
 
-    def dx_put(half, blk):
-        return pltpu.make_async_copy(dx_all.at[half, blk], dx_hbm.at[half, blk], dx_sem.at[half, blk])
-
-    gain = jnp.concatenate([gain_t[...]] * (half_rows // dim), axis=1)
-    for half in (0, 1):
-        xv = x_t[half]
-        inv = inv_r[half]
-        rows = slice(half * half_rows, (half + 1) * half_rows)
-        scaled = rs[steps, half, 1] * gain
-        mean = jnp.mean(xv * scaled, axis=0, keepdims=True)
-        dx = inv * (scaled - xv * inv * inv * mean)
-        dx = dout_ref[rows, :].astype(F32) + dx.T
-        dx_all[half, me] = dx.astype(BF16)
-        gather_begin(dx_all, e_sems, half)
-        dx_put(half, me).start()
-    for half in (0, 1):
-        rows = slice(half * half_rows, (half + 1) * half_rows)
-        out_ref[rows, :] = (x_t[half] + rs[steps, half, 0]).T.astype(BF16)
-
-    puts[4].start()
+    def finish_out():
+        for half in (0, 1):
+            rows = slice(half * half_rows, (half + 1) * half_rows)
+            r_copy(half, 0, steps - 1).wait_recv()
+            y = rs[steps, half, 0] + (parts[4 + half, 0] + precv[0, half, 0])
+            out_ref[rows, :] = (x_t[half] + y).T.astype(BF16)
+        puts[4].start()
 
     def pair_done(hop):
         for half in (0, 1):
-            pair_arrival(dx_all, ep_send, ep_recv, half, hop).wait_recv()
+            pair_arrival(dx_all, e_send, ep_recv, half, hop).wait_recv()
             dx_put(half, chip_at(half, hop) * 2 + 1 - core).start()
 
     def e_step(step, _):
@@ -407,6 +402,11 @@
         for half in (0, 1):
             dx_put(half, chip_at(half, step + 1) * 2 + core).start()
         pair_done(step)
+
+        @pl.when(step == min(2, steps - 1))
+        def _():
+            finish_out()
+
         return 0
 
     lax.fori_loop(0, steps, e_step, 0)
@@ -414,15 +414,10 @@
     for buf, sems in ((d_all, d_sems), (n_all, n_sems)):
         gather_drain(buf, sems)
 
-    def drain(step, _):
-        for half in (0, 1):
-            for piece in range(pieces):
-                x_copy(half, step, piece).wait_send()
-            for val in (0, 1):
-                r_copy(half, val, step).wait_send()
-        return 0
-
-    lax.fori_loop(0, steps, drain, 0)
+    sent = xs.at[:, pl.ds(0, steps)]
+    remote(sent, sent, x_send.at[0], x_recv.at[0, 0, 0], partner).wait_send()
+    sent = rs.at[pl.ds(0, steps)]
+    remote(sent, sent, r_send.at[0], r_recv.at[0, 0, 0], partner).wait_send()
     for half in (0, 1):
         for order in (chips - 2, chips - 1):
             p_copy(half, (order + half) % chips).wait_send()
@@ -431,12 +426,7 @@
     pair_done(steps)
     gather_drain(dx_all, e_sems)
 
-    def put_wait(blk, _):
-        for half in (0, 1):
-            dx_put(half, blk).wait()
-        return 0
-
-    lax.fori_loop(0, 2 * chips, put_wait, 0)
+    pltpu.make_async_copy(dx_all, dx_hbm, dx_sem.at[0]).wait()
 
 
 def row_tiles(hidden):
@@ -459,8 +449,7 @@
     groups = tokens // dim
 
     def gather_sems(pieces):
-        ring, pair = (2, chips - 1, pieces), (2, chips)
-        return [dma(ring), dma(ring), dma(pair), dma(pair)]
+        return [dma((2,)), dma((2, chips - 1, pieces)), dma((2, chips))]
 
     results = (
         jax.ShapeDtypeStruct((rows, dim), BF16),
@@ -491,14 +480,14 @@
             pltpu.VMEM((2, devs, dim, half), BF16),
             pltpu.VMEM((2, devs, dim, half), BF16),
             *[pltpu.VMEM((hidden, sub), BF16)] * 4,
-            pltpu.VMEM((5, 2, dim, half), F32),
+            pltpu.VMEM((6, 2, dim, half), F32),
             pltpu.VMEM((chips, 2, 2, dim, half), F32),
             pltpu.VMEM((chips, 2, 2, dim, half), F32),
-            dma((3,)), dma((5,)), dma((2, devs)),
-            dma((2, chips - 1, 2)), dma((2, chips - 1, 2)),
-            *gather_sems(1), *gather_sems(2), *gather_sems(4),
+            dma((3,)), dma((5,)), dma((1,)),
+            dma((1,)), dma((2, chips - 1, 2)),
+            *gather_sems(2), *gather_sems(2), *gather_sems(4),
             dma((chips, 2)), dma((chips, 2)),
-            dma((chips - 1, 2, 2)), dma((chips - 1, 2, 2)),
+            dma((1,)), dma((chips - 1, 2, 2)),
         ],
         compiler_params=pltpu.CompilerParams(
             collective_id=0, has_side_effects=True, vmem_limit_bytes=67043328,
@@ -511,8 +500,8 @@
 
 def scatter_kernel(extra, list_hbm, count_hbm, dx_ref, *refs):
     extra_in, grad_ref, extra_out = refs[:extra], refs[extra], refs[extra + 1:2 * extra + 1]
-    acc, dx_in, dx_f32, list_ref, count_ref, in_sem, ex_sem, small_sem = refs[2 * extra + 1:2 * extra + 9]
-    extra_buf = refs[2 * extra + 9:]
+    acc, acc_odd, dx_in, dx_f32, list_ref, count_ref, in_sem, ex_sem, small_sem = refs[2 * extra + 1:2 * extra + 10]
+    extra_buf = refs[2 * extra + 10:]
     blocks, block = dx_in.shape[:2]
     groups = list_ref.shape[0]
     tokens = dx_f32.shape[0]
@@ -539,6 +528,7 @@
     for e in range(extra):
         take(e).start()
     acc[...] = jnp.zeros(acc.shape, F32)
+    acc_odd[...] = jnp.zeros(acc.shape, F32)
     conv = 128
 
     for b in range(blocks):
@@ -561,18 +551,29 @@
         def bunch(i, _):
             for j in range(BUNCH):
                 packed = list_ref[g, i * BUNCH + j]
-                acc[pl.ds(packed >> shift, 1), :] += dx_f32[pl.ds(packed & (tokens - 1), 1), :]
+                into = acc_odd if j % 2 else acc
+                into[pl.ds(packed >> shift, 1), :] += dx_f32[pl.ds(packed & (tokens - 1), 1), :]
             return 0
 
         lax.fori_loop(0, count_ref[0, g], bunch, 0)
         return 0
 
     lax.fori_loop(0, groups, group, 0)
-    copy = pltpu.make_async_copy(acc.at[pl.ds(0, shard_rows)], grad_ref, in_sem.at[0])
-    copy.start()
+    cut = -(-shard_rows // (8 * blocks)) * 8
+
+    def flush(b):
+        rows = pl.ds(b * cut, min(cut, shard_rows - b * cut))
+        return pltpu.make_async_copy(acc.at[rows], grad_ref.at[rows], in_sem.at[b])
+
+    used = [b for b in range(blocks) if b * cut < shard_rows]
+    for b in used:
+        rows = slice(b * cut, min((b + 1) * cut, shard_rows))
+        acc[rows] = acc[rows] + acc_odd[rows]
+        flush(b).start()
     for e in range(extra):
         give(e).wait()
-    copy.wait()
+    for b in used:
+        flush(b).wait()
 
 
 def scatter_rows(shard_rows, lists, counts, dx_all, others):
@@ -588,6 +589,7 @@
         out_specs=(hbm,) * (1 + extra),
         scratch_shapes=[
             pltpu.VMEM((shard_rows + 8, dim), F32),
+            pltpu.VMEM((shard_rows + 8, dim), F32),
             pltpu.VMEM((blocks, tokens // blocks, dim), BF16),
             pltpu.VMEM((tokens, dim), F32),
             pltpu.SMEM(lists.shape, jnp.int32),

time: 217 us -> 206 us (0.949)
  Pallas kernels: 217 us -> 205 us
    pallas_call x1, Pallas kernels: 204 us -> 193 us  [run_block(): pl.pallas_call(functools.partial(block_kernel, chips, row_tiles(hidden)),...]
where the time goes in v4:
time: 206 us
  Pallas kernels  205 us (100%)
    pallas_call x1, Pallas kernels, run_block(): pl.pallas_call(functools.partial(block_kernel, chips, row_tiles(hidden)),...  193 us
    pallas_call x1, Pallas kernels, scatter_rows(): pl.pallas_call(functools.partial(scatter_kernel, extra), out_shape=tuple(...  11.8 us

profile of v4, /device:TPU:21, one launch (start us, length us, event | category | flops | bytes accessed | tf_op | source)
XLA Modules:
  0.0 205.6 jit_solution(11665169959130970353)
XLA Ops:
  0.6 193.1 %block.1 = (bf16[1024,128]{1,0:T(8,128)(2,1)}, f32[1184,128]{1,0:T(8,128)}, f32[1184,128]{1,0:T(8,128)}, bf16[2,16,512,128]{3,2,1,0:T(8,128)(2,1)}, s32[128,128]{1,0:T(8,128)}, /*index=5*/s32[8,128]{1,0:T(8,128)}) custom-call(s32[16384]{0:T(1024)} %ids_ref.1, s32[128,128]{1,0:T(8,128)} %bitcast.8, bf16[9504,128]{1,0:T(8,128)(2,1)} %table_hbm.1, ...), custom_call_target="tpu_custom_call" | custom-call | flops 29796335616 | bytes 16777216 | tf_op jit(solution)/shard_map/block/pallas_call | solution.py:463
  193.7 11.8 %scatter.1 = (f32[9504,128]{1,0:T(8,128)}, bf16[1024,128]{1,0:T(8,128)(2,1)}, f32[1184,128]{1,0:T(8,128)}, f32[1184,128]{1,0:T(8,128)}) custom-call(s32[128,128]{1,0:T(8,128)} %get-tuple-element.14.list_hbm, s32[8,128]{1,0:T(8,128)} %get-tuple-element.15.count_hbm, bf16[16384,128]{1,0:T(8,128)(2,1)} %bitcast.5, bf16[1024,128]{1,0:T(8,128)(2,1)} %get-tuple-element.17.refs_0_, ...), custom_call_target="tpu_custom_call" | custom-call | tf_op jit(solution)/shard_map/scatter/pallas_call | solution.py:585
